TPU v7x, 256 devices: a 8x8x2 block of a 8x8x16 slice. The times are simulated.
256 devices in a mesh: groups: 2 (over z), ctx: 128 (over y, x, core).
Axes of the slice: x: 8, y: 8, z: 2, core: 2. Of those that a mesh axis runs over, the one named last changes fastest.
The devices are a block of a 8x8x16 slice.
Arguments:
- query_states: bfloat16 [131072, 32, 128], P(('groups', 'ctx')), parts along dimension 0, may hold values from -20 to 20
- key_states: bfloat16 [131072, 8, 128], P(('groups', 'ctx')), parts along dimension 0, may hold values from -4 to 4
- value_states: bfloat16 [131072, 8, 128], P(('groups', 'ctx')), parts along dimension 0, may hold values from -6 to 6
- vert_blocks: int32 [16, 4], P('groups'), parts along dimension 0, may hold values from 0 to 511, as said below
- vert_count: int32 [16], P('groups'), parts along dimension 0, may hold values from 1 to 4, as said below
- slash_offsets: int32 [16, 4], P('groups'), parts along dimension 0, may hold values from 0 to 8, as said below
- slash_count: int32 [16], P('groups'), parts along dimension 0, may hold values from 1 to 4, as said below
Outputs:
- attended: bfloat16 [131072, 32, 128], P(('groups', 'ctx')), parts along dimension 0
There are 2 independent parts, one for each index of `groups`. A program takes and returns all parts, laid end to end along the dimension named above; each array names one. Nothing has to cross between parts.
Inputs may be any that keep to these rules, and one draw needn't show every extreme that they name: `vert_blocks`: the 4 entries of each head are distinct; in some head the first entry lies in one of the first 4 blocks. `vert_count`: some head uses all 4 entries. `slash_offsets`: the 4 entries of each head are distinct and the first is 0. `slash_count`: some head uses all 4 entries.
All inputs are finite; a program needn't handle non-finite values.
Results may differ from a plain program's by a relative error of at most 0.0048.
Values may be sent and summed in bfloat16 or wider, within the bound.
No kernel may reach another device: no remote copies, remote signals or barrier semaphores. Data moves between devices by JAX's collectives and lax.ppermute only.
A program may use at most 128 MiB of HBM per device.

v0:
```python
import functools
import math

import jax
import jax.numpy as jnp
from jax import lax
from jax.experimental import pallas as pl
from jax.experimental.pallas import tpu as pltpu
from jax.sharding import Mesh, PartitionSpec as P


BLOCK = 128
SLOTS = 6
CORES = 2
PAIR = 2
ALL = ("y", "x", "core")


def shifted(x, by):
    size = lax.axis_size(ALL)
    pairs = [(i, i + by) for i in range(size) if 0 <= i + by < size]
    return lax.ppermute(x, ALL, pairs)


def whole_spec(x):
    return pl.BlockSpec(x.shape, lambda *_: (0,) * x.ndim)


def small_call(body, scalars, arrays, out_shape, scratch):
    return pl.pallas_call(
        body,
        grid_spec=pltpu.PrefetchScalarGridSpec(
            num_scalar_prefetch=len(scalars),
            grid=(1,),
            in_specs=[whole_spec(a) for a in arrays],
            out_specs=pl.BlockSpec(out_shape, lambda *_: (0,) * len(out_shape)),
            scratch_shapes=scratch,
        ),
        out_shape=jax.ShapeDtypeStruct(out_shape, arrays[0].dtype),
    )(*scalars, *arrays)


def each_tile(verts, counts, per_dev, n_vert, columns):
    for i in range(verts.shape[0]):
        block = verts[i]
        owner = block // per_dev
        used = (i % n_vert) < counts[i // n_vert]
        yield i, used, owner // columns, owner % columns, (i // n_vert) * per_dev + block % per_dev


def pick_body(verts, counts, place, pool, send, *, per_dev, n_vert, columns):
    seen = jnp.int32(0) - place[2] * SLOTS
    for _, used, row, col, tile in each_tile(verts, counts, per_dev, n_vert, columns):
        here = used & (col == place[1])

        @pl.when(here & (row == place[0]) & (seen >= 0) & (seen < SLOTS))
        def _():
            send[:, seen] = pool[tile]

        seen = seen + here.astype(jnp.int32)


def keep_body(verts, counts, place, got, send, *, per_dev, n_vert, columns):
    seen = jnp.int32(0) - place[2] * SLOTS
    for _, used, row, col, _ in each_tile(verts, counts, per_dev, n_vert, columns):
        here = used & (col == place[1])

        @pl.when(here & (seen >= 0) & (seen < SLOTS))
        def _():
            piece = got[row, seen]
            for i in range(send.shape[0]):
                send[i, seen] = piece

        seen = seen + here.astype(jnp.int32)


def merge_body(verts, counts, place, same, other, old, out, seen, *, per_dev, n_vert, columns):
    half = out.shape[0]
    core = place[1] % CORES
    out[...] = old[...]
    for i in range(columns):
        seen[i] = -place[2] * SLOTS
    for i, used, _, col, _ in each_tile(verts, counts, per_dev, n_vert, columns):
        slot = seen[col]
        seen[col] = slot + used.astype(jnp.int32)
        wanted = used & (slot >= 0) & (slot < SLOTS) & (core == i // half)

        @pl.when(wanted & (col % CORES == core))
        def _():
            out[i % half] = same[col // CORES, slot]

        @pl.when(wanted & (col % CORES != core))
        def _():
            out[i % half] = other[col // CORES, slot]


def spread_vertical(pool, verts, counts, device, per_dev, n_vert, rider):
    rows_y, cols_x = lax.axis_size("y"), lax.axis_size("x")
    columns = cols_x * CORES
    n_tiles, tile_rows, width = pool.shape
    piece = tile_rows // rows_y
    half = len(verts) // CORES
    static = dict(per_dev=per_dev, n_vert=n_vert, columns=columns)
    pool = pool.reshape(n_tiles, rows_y, piece, width)
    swap = lambda x: lax.ppermute(x, "core", [(0, 1), (1, 0)])

    def turn(t, kept, rider):
        place = jnp.stack((device // columns, device % columns, t)).astype(jnp.int32)
        scalars = (verts, counts, place)
        shape_y = (rows_y, SLOTS, piece, width)
        shape_x = (cols_x, SLOTS, piece, width)
        send = small_call(functools.partial(pick_body, **static), scalars, (pool,), shape_y, [])
        got = lax.all_to_all(send, "y", 0, 0, tiled=True)
        got, rider = lax.optimization_barrier((got, rider))
        send = small_call(functools.partial(keep_body, **static), scalars, (got,), shape_x, [])
        same = lax.all_to_all(send, "x", 0, 0, tiled=True)
        merged = small_call(
            functools.partial(merge_body, **static), scalars, (same, swap(same), kept),
            kept.shape, [pltpu.SMEM((columns,), jnp.int32)],
        )
        return merged, rider

    used = (jnp.arange(n_vert)[None, :] < counts[:, None]).reshape(-1)
    column_of = (verts // per_dev) % columns
    load = jnp.sum((column_of[None, :] == jnp.arange(columns)[:, None]) & used, axis=1)
    turns = (jnp.max(load) + SLOTS - 1) // SLOTS
    first, rider = turn(jnp.int32(0), jnp.zeros((half, piece, width), pool.dtype), rider)
    held = lax.while_loop(
        lambda c: c[0] < turns, lambda c: (c[0] + 1, turn(c[0], c[1], ())[0]),
        (jnp.int32(1), first),
    )[1]
    mine = lax.all_to_all(
        jnp.broadcast_to(held, (rows_y, *held.shape)), "y", 0, 0, tiled=True
    )
    return mine, swap(mine), rider


def fill_ones(vals, dim):
    vals[:, :, :, dim:] = jnp.ones((*vals.shape[:3], dim), vals.dtype)


def window_body(
    verts, vert_count, slashes, slash_count, place, q_ref, own_ref, core_ref, chip_ref, far_ref,
    part_ref, stat_ref, keys, vals, lists, *, n_vert, n_slash, per_dev,
):
    step = pl.program_id(0)
    group, _, dim = q_ref.shape[1:]
    scale = math.log2(math.e) / math.sqrt(dim)
    core = place[0] % CORES
    most = n_slash + min(n_vert, per_dev - 1)

    @pl.when(step == 0)
    def _():
        fill_ones(vals, dim)

    for hh in range(PAIR):
        def put(at, tile):
            keys[hh, at] = tile[:BLOCK]
            vals[hh, at, :, :dim] = tile[BLOCK:]

        for i in range(per_dev):
            put(i, far_ref[hh, i])
            put(2 * per_dev + i, own_ref[hh, i])

        @pl.when(core == 1)
        def _():
            for i in range(per_dev):
                put(per_dev + i, core_ref[hh, i])

        @pl.when(core == 0)
        def _():
            for i in range(per_dev):
                put(per_dev + i, chip_ref[hh, i])

    row = lax.broadcasted_iota(jnp.int32, (BLOCK, BLOCK), 0)
    col = lax.broadcasted_iota(jnp.int32, (BLOCK, BLOCK), 1)
    causal = jnp.concatenate([col <= row] * 2, axis=0)
    lane = col // (dim // group)

    def block(l, carry):
        qblock = place[0] * per_dev + l
        for hh in range(PAIR):
            head = step * PAIR + hh
            n_used = vert_count[head]
            count = jnp.int32(1)
            for i in range(n_slash):
                offset = slashes[head * n_slash + i]
                block_at = qblock - offset
                ok = (i < slash_count[head]) & (offset > 0) & (block_at >= 0)
                for j in range(n_vert):
                    ok = ok & jnp.logical_not((j < n_used) & (verts[head * n_vert + j] == block_at))
                lists[count] = l - offset + 2 * per_dev
                count = count + ok.astype(jnp.int32)
            for j in range(n_vert):
                at = verts[head * n_vert + j] - place[0] * per_dev
                ok = (j < n_used) & (at >= 0) & (at < l)
                lists[count] = at + 2 * per_dev
                count = count + ok.astype(jnp.int32)

            def run(n):
                at = [2 * per_dev + l] + [lists[i] for i in range(1, n)]
                k = jnp.concatenate([keys[hh, i] for i in at], axis=0)
                v = jnp.concatenate([vals[hh, i] for i in at], axis=0)
                rows = pl.ds(l * BLOCK, BLOCK)
                stat = None
                for r in range(0, group, 2):
                    q = q_ref[hh, r : r + 2, rows, :].reshape(2 * BLOCK, dim)
                    s = lax.dot_general(
                        q, k, (((1,), (1,)), ((), ())), preferred_element_type=jnp.float32
                    )
                    parts = [s[:, i * BLOCK : (i + 1) * BLOCK] for i in range(n)]
                    parts[0] = jnp.where(causal, parts[0], -jnp.inf)
                    top = functools.reduce(jnp.maximum, parts)
                    top = jnp.max(top, axis=-1, keepdims=True) * scale
                    p = jnp.concatenate(
                        [jnp.exp2(x * scale - top).astype(jnp.bfloat16) for x in parts], axis=1
                    )
                    o = jnp.dot(p, v, preferred_element_type=jnp.float32)
                    part_ref[hh, r : r + 2, rows, :] = (o[:, :dim] / o[:, dim:]).reshape(
                        2, BLOCK, dim
                    )
                    logs = top + jnp.log2(o[:, dim:])
                    for i in range(2):
                        mine = logs[i * BLOCK : (i + 1) * BLOCK]
                        stat = mine if stat is None else jnp.where(lane == r + i, mine, stat)
                stat_ref[hh, rows, :] = stat

            for n in range(1, most + 1):
                pl.when(count == n)(functools.partial(run, n))
        return carry

    lax.fori_loop(0, per_dev, block, 0)


def vertical_body(
    verts, vert_count, place, q_ref, part_ref, stat_ref, mine_ref, theirs_ref, out_ref,
    keys, vals, wide, s0, s1, p0, p1, t0, t1, *, n_vert, per_dev, half, chunk,
):
    step = pl.program_id(0)
    group, rows, dim = q_ref.shape[1:]
    scale = math.log2(math.e) / math.sqrt(dim)
    core = place[0] % CORES
    chunks = rows // chunk
    heads = PAIR * group

    @pl.when(step == 0)
    def _():
        fill_ones(vals, dim)

    for hh in range(PAIR):
        first = (step * PAIR + hh) * n_vert

        def take(source):
            count = jnp.int32(0)
            for j in range(n_vert):
                ok = (j < vert_count[step * PAIR + hh]) & (
                    verts[first + j] < place[0] * per_dev
                )

                @pl.when(ok)
                def _():
                    tile = source[:, first % half + j].reshape(2 * BLOCK, dim)
                    keys[hh, count] = tile[:BLOCK]
                    vals[hh, count, :, :dim] = tile[BLOCK:]

                count = count + ok.astype(jnp.int32)

        pl.when(first // half == core)(lambda: take(mine_ref))
        pl.when(first // half != core)(lambda: take(theirs_ref))
        count = jnp.int32(0)
        for j in range(n_vert):
            ok = (j < vert_count[step * PAIR + hh]) & (verts[first + j] < place[0] * per_dev)
            count = count + ok.astype(jnp.int32)

        def store(i, r, value):
            wide[pl.ds(i * chunk * heads + hh * group + r, chunk, stride=heads), :] = value

        def run(n):
            wide_keys = n * BLOCK

            def stages(i, s_in, s_out, p_in, p_out, t_in, t_out):
                at = jnp.minimum(i, chunks - 1)
                q = q_ref[hh, :, pl.ds(at * chunk, chunk), :].reshape(group * chunk, dim)
                k = keys[hh, :n].reshape(wide_keys, dim)
                s_in[:, :wide_keys] = lax.dot_general(
                    q, k, (((1,), (1,)), ((), ())), preferred_element_type=jnp.float32
                ) * scale
                parts = [s_out[:, j * BLOCK : (j + 1) * BLOCK] for j in range(n)]
                top = jnp.max(functools.reduce(jnp.maximum, parts), axis=-1, keepdims=True)
                for j in range(n):
                    p_in[:, j * BLOCK : (j + 1) * BLOCK] = jnp.exp2(parts[j] - top).astype(
                        jnp.bfloat16
                    )
                t_in[...] = jnp.broadcast_to(top, t_in.shape)
                at = jnp.clip(i - 2, 0, chunks - 1)
                v = vals[hh, :n].reshape(wide_keys, 2 * dim)
                o = jnp.dot(p_out[:, :wide_keys], v, preferred_element_type=jnp.float32)
                stat = stat_ref[hh, pl.ds(at * chunk, chunk), :]
                for r in range(group):
                    some = slice(r * chunk, (r + 1) * chunk)
                    lane = r * (dim // group)
                    logs = jnp.broadcast_to(stat[:, lane : lane + 1], (chunk, dim))
                    new = t_out[some]
                    most = jnp.maximum(logs, new)
                    before, after = jnp.exp2(logs - most), jnp.exp2(new - most)
                    whole = part_ref[hh, r, pl.ds(at * chunk, chunk), :] * before
                    whole = whole + o[some, :dim] * after
                    store(at, r, whole / (before + o[some, dim:] * after))

            def two(i, carry):
                stages(2 * i, s0, s1, p1, p0, t1, t0)
                stages(2 * i + 1, s1, s0, p0, p1, t0, t1)
                return carry

            lax.fori_loop(0, (chunks + 2) // 2, two, 0)

        @pl.when(count == 0)
        def _():
            def copy(i, carry):
                for r in range(group):
                    store(i, r, part_ref[hh, r, pl.ds(i * chunk, chunk), :])
                return carry

            lax.fori_loop(0, chunks, copy, 0)

        for n in range(1, n_vert + 1):
            pl.when(count == n)(functools.partial(run, n))

    def write(i, carry):
        some = wide[pl.ds(i * chunk * heads, chunk * heads), :]
        out_ref[pl.ds(i * chunk, chunk)] = some.reshape(chunk, heads, dim).astype(out_ref.dtype)
        return carry

    lax.fori_loop(0, chunks, write, 0)


def cost(queries, tiles):
    size = math.prod(queries.shape)
    return pl.CostEstimate(
        flops=4 * size * BLOCK * tiles, transcendentals=size * tiles, bytes_accessed=8 * size
    )


def attend_window(queries, own, core_kv, chip_kv, far, verts, vert_count, slashes, slash_count, device):
    heads, group, rows, dim = queries.shape
    per_dev = own.shape[1]
    n_vert = len(verts) // heads
    n_slash = len(slashes) // heads
    kv_spec = pl.BlockSpec((PAIR, *own.shape[1:]), lambda h, *_: (h, 0, 0, 0))
    q_spec = pl.BlockSpec((PAIR, group, rows, dim), lambda h, *_: (h, 0, 0, 0))
    return pl.pallas_call(
        functools.partial(window_body, n_vert=n_vert, n_slash=n_slash, per_dev=per_dev),
        grid_spec=pltpu.PrefetchScalarGridSpec(
            num_scalar_prefetch=5,
            grid=(heads // PAIR,),
            in_specs=[q_spec, kv_spec, kv_spec, kv_spec, kv_spec],
            out_specs=[q_spec, pl.BlockSpec((PAIR, rows, dim), lambda h, *_: (h, 0, 0))],
            scratch_shapes=[
                pltpu.VMEM((PAIR, 3 * per_dev, BLOCK, dim), own.dtype),
                pltpu.VMEM((PAIR, 3 * per_dev, BLOCK, 2 * dim), own.dtype),
                pltpu.SMEM((n_vert + n_slash + 1,), jnp.int32),
            ],
        ),
        out_shape=[
            jax.ShapeDtypeStruct(queries.shape, jnp.float32),
            jax.ShapeDtypeStruct((heads, rows, dim), jnp.float32),
        ],
        cost_estimate=cost(queries, n_slash),
        name="window",
    )(
        verts, vert_count, slashes, slash_count, device.reshape(1),
        queries, own, core_kv, chip_kv, far,
    )


def attend_vertical(queries, part, stat, mine, theirs, verts, vert_count, device, per_dev):
    heads, group, rows, dim = queries.shape
    n_vert = len(verts) // heads
    chunk = rows // 8
    lines = group * chunk
    q_spec = pl.BlockSpec((PAIR, group, rows, dim), lambda h, *_: (h, 0, 0, 0))
    scores = pltpu.VMEM((lines, n_vert * BLOCK), jnp.float32)
    powers = pltpu.VMEM((lines, n_vert * BLOCK), queries.dtype)
    tops = pltpu.VMEM((lines, dim), jnp.float32)
    return pl.pallas_call(
        functools.partial(
            vertical_body, n_vert=n_vert, per_dev=per_dev, half=mine.shape[1], chunk=chunk
        ),
        grid_spec=pltpu.PrefetchScalarGridSpec(
            num_scalar_prefetch=3,
            grid=(heads // PAIR,),
            in_specs=[
                q_spec, q_spec, pl.BlockSpec((PAIR, rows, dim), lambda h, *_: (h, 0, 0)),
                whole_spec(mine), whole_spec(theirs),
            ],
            out_specs=pl.BlockSpec((rows, PAIR * group, dim), lambda h, *_: (0, h, 0)),
            scratch_shapes=[
                pltpu.VMEM((PAIR, n_vert, BLOCK, dim), queries.dtype),
                pltpu.VMEM((PAIR, n_vert, BLOCK, 2 * dim), queries.dtype),
                pltpu.VMEM((rows * PAIR * group, dim), jnp.float32),
                scores, scores, powers, powers, tops, tops,
            ],
        ),
        out_shape=jax.ShapeDtypeStruct((rows, heads * group, dim), queries.dtype),
        cost_estimate=cost(queries, n_vert),
        name="vertical",
    )(verts, vert_count, device.reshape(1), queries, part, stat, mine, theirs)


def local(
    query_states, key_states, value_states, vert_blocks, vert_count, slash_offsets, slash_count
):
    rows_dev, q_heads, head_dim = query_states.shape
    kv_heads = key_states.shape[1]
    group_size = q_heads // kv_heads
    per_dev = rows_dev // BLOCK
    n_vert = vert_blocks.shape[1]
    device = lax.axis_index(ALL).astype(jnp.int32)
    own = jnp.stack((key_states, value_states)).reshape(2, per_dev, BLOCK, kv_heads, head_dim)
    own = jnp.transpose(own, (3, 1, 0, 2, 4)).reshape(kv_heads, per_dev, 2 * BLOCK, head_dim)
    far = shifted(own, 2)
    core_kv = lax.ppermute(own, "core", [(0, 1)])
    chip_kv = lax.ppermute(far, "core", [(1, 0)])
    verts = vert_blocks.reshape(-1)
    queries = jnp.moveaxis(query_states.reshape(rows_dev, kv_heads, group_size, head_dim), 0, 2)
    mine, theirs, queries = spread_vertical(
        own.reshape(kv_heads * per_dev, 2 * BLOCK, head_dim),
        verts, vert_count, device, per_dev, n_vert, queries,
    )
    part, stat = attend_window(
        queries, own, core_kv, chip_kv, far,
        verts, vert_count, slash_offsets.reshape(-1), slash_count, device,
    )
    return attend_vertical(
        queries, part, stat, mine, theirs, verts, vert_count, device, per_dev
    )


def solution(mesh):
    groups, size = mesh.shape["groups"], mesh.shape["ctx"]
    side = math.isqrt(size // CORES)
    parts = Mesh(
        mesh.devices.reshape(groups, size // (CORES * side), side, CORES), ("groups", *ALL)
    )
    rows = P(("groups", *ALL), None, None)
    in_specs = (rows, rows, rows, P("groups", None), P("groups"), P("groups", None), P("groups"))
    return jax.shard_map(local, mesh=parts, in_specs=in_specs, out_specs=rows, check_vma=False)
```

profile of v0, /device:TPU:737, one launch (start us, length us, event | category | flops | bytes accessed | tf_op | source)
XLA Modules:
  0.0 184.0 jit_solution(17426169597152032933)
XLA Ops:
  0.0 0.0 copy-start.6
  0.0 0.8 copy.18
  0.8 0.1 reshape.75.verts
  0.9 0.0 copy-start.8
  0.9 2.5 %copy_dynamic-update-slice_fusion.1 = bf16[2,4,128,8,128]{4,2,0,1,3:T(8,128)(2,1)} fusion(bf16[1,4,128,8,128]{4,3,2,1,0:T(8,128)(2,1)} %bitcast.24), kind=kLoop, calls=%fused_computation.2 | loop fusion | bytes 2097152
  3.4 0.0 copy-done.6
  3.4 1.2 copy_dynamic-update-slice_fusion
  4.6 0.6 pad_add_fusion.1.place
  5.2 0.0 copy-done.8
  5.2 3.0 %shard_map.73 = bf16[8,6,32,128]{3,2,1,0:T(8,128)(2,1)} custom-call(s32[32]{0:T(128)S(1)} %reshape.75.verts, s32[8]{0:T(128)S(1)} %copy-done.8, s32[3]{0:T(128)} %pad_add_fusion.1.place, bf16[32,8,32,128]{3,2,1,0:T(8,128)(2,1)} %bitcast.9.pool), custom_call_target="tpu_custom_call" | custom-call | tf_op jit(solution)/shard_map/pallas_call | solution.py:30
  8.3 5.3 %all-to-all-start.2 = ((bf16[8,6,32,128]{3,2,1,0:T(8,128)(2,1)}), bf16[8,6,32,128]{3,2,1,0:T(8,128)(2,1)S(1)}, u32[]{:S(2)}, u32[]{:S(2)}) async-start(bf16[8,6,32,128]{3,2,1,0:T(8,128)(2,1)} %shard_map.73), calls=%async_computation.2 | async-start | bytes 786432 | tf_op jit(solution)/shard_map/all_to_all | solution.py:113
  13.6 3.3 %collective-permute-start.2 = (bf16[8,4,256,128]{3,2,1,0:T(8,128)(2,1)}, bf16[8,4,256,128]{3,2,1,0:T(8,128)(2,1)}, u32[]{:S(2)}, u32[]{:S(2)}) collective-permute-start(bf16[8,4,256,128]{3,2,1,0:T(8,128)(2,1)} %bitcast.12.own_ref), channel_id=1, source_target_pairs={{0,2},{1,3},{2,4},{3,5},{4,6},{5,7},{6,8},{7,9},{8,10},{9,11},{10,... | collective-permute-start | bytes 6291464 | tf_op jit(solution)/shard_map/ppermute | solution.py:22
  16.8 5.8 %copy.21 = bf16[512,32,128]{2,0,1:T(8,128)(2,1)} copy(bf16[512,32,128]{2,1,0:T(8,128)(2,1)} %param.9) | data formatting | bytes 8388608 | tf_op args[0]
  22.6 47.0 %all-to-all-done.2.got = bf16[8,6,32,128]{3,2,1,0:T(8,128)(2,1)S(1)} async-done(((bf16[8,6,32,128]{3,2,1,0:T(8,128)(2,1)}), bf16[8,6,32,128]{3,2,1,0:T(8,128)(2,1)S(1)}, u32[]{:S(2)}, u32[]{:S(2)}) %all-to-all-start.2) | async-done | bytes 393248 | tf_op jit(solution)/shard_map/all_to_all | solution.py:113
  69.6 0.0 copy-start.4
  69.6 0.8 copy-done.4
  70.4 2.9 %shard_map.74 = bf16[8,6,32,128]{3,2,1,0:T(8,128)(2,1)} custom-call(s32[32]{0:T(128)S(1)} %reshape.75.verts, s32[8]{0:T(128)S(1)} %copy-done.8, s32[3]{0:T(128)} %pad_add_fusion.1.place, bf16[8,6,32,128]{3,2,1,0:T(8,128)(2,1)} %copy-done.4), custom_call_target="tpu_custom_call" | custom-call | tf_op jit(solution)/shard_map/pallas_call | solution.py:30
  73.3 16.9 %all_to_all.31.same = bf16[8,6,32,128]{3,2,1,0:T(8,128)(2,1)S(1)} all-to-all(bf16[8,6,32,128]{3,2,1,0:T(8,128)(2,1)} %shard_map.74), channel_id=1, replica_groups=mesh['groups'=2,'y'=8,'x'=8,'core'=2] {'x'}, dimensions={0} | all-to-all | bytes 786432 | tf_op jit(solution)/shard_map/all_to_all | solution.py:116
  90.2 0.0 copy-start.3
  90.2 2.1 %collective-permute-start.4 = (bf16[8,6,32,128]{3,2,1,0:T(8,128)(2,1)S(1)}, bf16[8,6,32,128]{3,2,1,0:T(8,128)(2,1)S(1)}, u32[]{:S(2)}, u32[]{:S(2)}) collective-permute-start(bf16[8,6,32,128]{3,2,1,0:T(8,128)(2,1)S(1)} %all_to_all.31.same), channel_id=1, source_target_pairs={{0,1},{1,0},{2,3},{3,2},{4,5},{5,4},{6,7},{7,6},{8,9},{9,8},{10,11... | collective-permute-start | bytes 1179656 | tf_op jit(solution)/shard_map/ppermute | solution.py:105
  92.3 0.1 iota_compare_fusion.1
  92.4 0.1 lt.48
  92.5 0.1 convert_reduce_fusion
  92.6 0.7 reduce_max.9
  94.0 0.0 collective-permute-done.4.other
  94.0 0.0 copy-start.7
  94.0 0.7 broadcast_in_dim.4.old
  94.8 0.0 copy-done.3
  94.8 0.1 copy-done.7
  94.8 2.9 %shard_map.75 = bf16[16,32,128]{2,1,0:T(8,128)(2,1)S(1)} custom-call(s32[32]{0:T(128)S(1)} %reshape.75.verts, s32[8]{0:T(128)S(1)} %copy-done.8, s32[3]{0:T(128)} %pad_add_fusion.1.place, bf16[8,6,32,128]{3,2,1,0:T(8,128)(2,1)} %copy-done.3, bf16[8,6,32,128]{3,2,1,0:T(8,128)(2,1)} %copy-done.7, bf16[16,32,128]{2,1,0:T(8,128)(2,1)} %broadcast_in_dim.4.old), custom_call_target="tpu_custom_call" | custom-call | tf_op jit(solution)/shard_map/pallas_call | solution.py:30
  97.8 0.0 copy-start.9
  97.8 1.2 broadcast_in_dim.5
  99.0 6.8 %all-to-all-start.4 = ((bf16[8,16,32,128]{3,2,1,0:T(8,128)(2,1)}), bf16[8,16,32,128]{3,2,1,0:T(8,128)(2,1)S(1)}, u32[]{:S(2)}, u32[]{:S(2)}) async-start(bf16[8,16,32,128]{3,2,1,0:T(8,128)(2,1)} %broadcast_in_dim.5), calls=%async_computation.4 | async-start | bytes 2097152 | tf_op jit(solution)/shard_map/all_to_all | solution.py:132
  105.7 1.3 collective-permute-start.1
  107.0 0.0 collective-permute-done.2.far_ref
  107.0 5.7 %collective-permute-start.3 = (bf16[8,4,256,128]{3,2,1,0:T(8,128)(2,1)}, bf16[8,4,256,128]{3,2,1,0:T(8,128)(2,1)}, u32[]{:S(2)}, u32[]{:S(2)}) collective-permute-start(bf16[8,4,256,128]{3,2,1,0:T(8,128)(2,1)} %collective-permute-done.2.far_ref), channel_id=1, source_target_pairs={{1,0},{3,2},{5,4},{7,6},{9,8},{11,10},{13,12},{15,14},{17,16},{19,... | collective-permute-start | bytes 6291464 | tf_op jit(solution)/shard_map/ppermute | solution.py:423
  112.8 18.8 %all-to-all-done.4.mine_ref = bf16[8,16,32,128]{3,2,1,0:T(8,128)(2,1)S(1)} async-done(((bf16[8,16,32,128]{3,2,1,0:T(8,128)(2,1)}), bf16[8,16,32,128]{3,2,1,0:T(8,128)(2,1)S(1)}, u32[]{:S(2)}, u32[]{:S(2)}) %all-to-all-start.4) | async-done | bytes 1048608 | tf_op jit(solution)/shard_map/all_to_all | solution.py:132
  131.5 0.0 copy-start.2
  131.5 0.6 collective-permute-start.5
  132.1 0.0 copy-done.9
  132.1 0.1 copy.22
  132.2 0.6 reshape.78.slashes
  132.8 0.0 collective-permute-done.1.core_ref
  132.8 0.0 collective-permute-done.3.chip_ref
  132.8 26.8 %window.1 = (f32[8,4,512,128]{3,2,1,0:T(8,128)}, f32[8,512,128]{2,1,0:T(8,128)}) custom-call(s32[32]{0:T(128)S(1)} %get-tuple-element.368, s32[8]{0:T(128)S(1)} %get-tuple-element.369, s32[32]{0:T(128)} %reshape.78.slashes, s32[8]{0:T(128)} %slash_count.1, s32[1]{0:T(128)} %bitcast.3.place, bf16[8,4,512,128]{3,2,1,0:T(8,128)(2,1)} %bitcast.22, ...), custom_call_target="tpu_custom_call" | custom-call | flops 4294967296 | bytes 16777216 | tf_op jit(solution)/shard_map/window/pallas_call | solution.py:351
  159.7 0.0 copy-done.2
  159.7 0.0 collective-permute-done.5.theirs_ref
  159.7 0.0 copy-start.5
  159.7 1.0 copy-done.5
  160.7 23.3 %vertical.1 = bf16[512,32,128]{2,1,0:T(8,128)(2,1)} custom-call(s32[32]{0:T(128)S(1)} %get-tuple-element.368, s32[8]{0:T(128)S(1)} %get-tuple-element.369, s32[1]{0:T(128)} %bitcast.3.place, bf16[8,4,512,128]{3,2,1,0:T(8,128)(2,1)} %bitcast.23, f32[8,4,512,128]{3,2,1,0:T(8,128)} %get-tuple-element.261.part_ref, f32[8,512,128]{2,1,0:T(8,128)} %get-tuple-element.262.stat_ref, ...), custom_call_target="tpu_custom_call" | custom-call | flops 4294967296 | bytes 16777216 | tf_op jit(solution)/shard_map/vertical/pallas_call | solution.py:385
  (2 shorter events, 0.0 us)
Async XLA Ops:
  0.0 3.4 %copy-start.6 = (bf16[512,8,128]{2,1,0:T(8,128)(2,1)S(1)}, bf16[512,8,128]{2,1,0:T(8,128)(2,1)}, u32[]{:S(2)}) copy-start(bf16[512,8,128]{2,1,0:T(8,128)(2,1)} %param.11) | copy-start | bytes 3145732
  0.9 4.3 %copy-start.8 = (s32[8]{0:T(128)S(1)}, s32[8]{0:T(128)}, u32[]{:S(2)}) copy-start(s32[8]{0:T(128)} %vert_count.3) | copy-start | bytes 100
  8.3 61.4 %all-to-all-start.2 = ((bf16[8,6,32,128]{3,2,1,0:T(8,128)(2,1)}), bf16[8,6,32,128]{3,2,1,0:T(8,128)(2,1)S(1)}, u32[]{:S(2)}, u32[]{:S(2)}) async-start(bf16[8,6,32,128]{3,2,1,0:T(8,128)(2,1)} %shard_map.73), calls=%async_computation.2 | async-start | bytes 786432 | tf_op jit(solution)/shard_map/all_to_all | solution.py:113
  13.6 93.5 %collective-permute-start.2 = (bf16[8,4,256,128]{3,2,1,0:T(8,128)(2,1)}, bf16[8,4,256,128]{3,2,1,0:T(8,128)(2,1)}, u32[]{:S(2)}, u32[]{:S(2)}) collective-permute-start(bf16[8,4,256,128]{3,2,1,0:T(8,128)(2,1)} %bitcast.12.own_ref), channel_id=1, source_target_pairs={{0,2},{1,3},{2,4},{3,5},{4,6},{5,7},{6,8},{7,9},{8,10},{9,11},{10,... | collective-permute-start | bytes 6291464 | tf_op jit(solution)/shard_map/ppermute | solution.py:22
  69.6 0.8 copy-start.4
  90.2 4.6 %copy-start.3 = (bf16[8,6,32,128]{3,2,1,0:T(8,128)(2,1)}, bf16[8,6,32,128]{3,2,1,0:T(8,128)(2,1)S(1)}, u32[]{:S(2)}) copy-start(bf16[8,6,32,128]{3,2,1,0:T(8,128)(2,1)S(1)} %all_to_all.31.same) | copy-start | bytes 1179652
  90.2 3.9 %collective-permute-start.4 = (bf16[8,6,32,128]{3,2,1,0:T(8,128)(2,1)S(1)}, bf16[8,6,32,128]{3,2,1,0:T(8,128)(2,1)S(1)}, u32[]{:S(2)}, u32[]{:S(2)}) collective-permute-start(bf16[8,6,32,128]{3,2,1,0:T(8,128)(2,1)S(1)} %all_to_all.31.same), channel_id=1, source_target_pairs={{0,1},{1,0},{2,3},{3,2},{4,5},{5,4},{6,7},{7,6},{8,9},{9,8},{10,11... | collective-permute-start | bytes 1179656 | tf_op jit(solution)/shard_map/ppermute | solution.py:105
  94.0 0.8 copy-start.7
  97.8 34.3 %copy-start.9 = (s32[8,4]{0,1:T(4,128)S(1)}, s32[8,4]{0,1:T(4,128)}, u32[]{:S(2)}) copy-start(s32[8,4]{0,1:T(4,128)} %param.14) | copy-start | bytes 388
  99.0 32.5 %all-to-all-start.4 = ((bf16[8,16,32,128]{3,2,1,0:T(8,128)(2,1)}), bf16[8,16,32,128]{3,2,1,0:T(8,128)(2,1)S(1)}, u32[]{:S(2)}, u32[]{:S(2)}) async-start(bf16[8,16,32,128]{3,2,1,0:T(8,128)(2,1)} %broadcast_in_dim.5), calls=%async_computation.4 | async-start | bytes 2097152 | tf_op jit(solution)/shard_map/all_to_all | solution.py:132
  105.7 27.1 %collective-permute-start.1 = (bf16[8,4,256,128]{3,2,1,0:T(8,128)(2,1)}, bf16[8,4,256,128]{3,2,1,0:T(8,128)(2,1)}, u32[]{:S(2)}, u32[]{:S(2)}) collective-permute-start(bf16[8,4,256,128]{3,2,1,0:T(8,128)(2,1)} %bitcast.12.own_ref), channel_id=1, source_target_pairs={{0,1},{2,3},{4,5},{6,7},{8,9},{10,11},{12,13},{14,15},{16,17},{18,... | collective-permute-start | bytes 6291464 | tf_op jit(solution)/shard_map/ppermute | solution.py:422
  107.0 25.8 %collective-permute-start.3 = (bf16[8,4,256,128]{3,2,1,0:T(8,128)(2,1)}, bf16[8,4,256,128]{3,2,1,0:T(8,128)(2,1)}, u32[]{:S(2)}, u32[]{:S(2)}) collective-permute-start(bf16[8,4,256,128]{3,2,1,0:T(8,128)(2,1)} %collective-permute-done.2.far_ref), channel_id=1, source_target_pairs={{1,0},{3,2},{5,4},{7,6},{9,8},{11,10},{13,12},{15,14},{17,16},{19,... | collective-permute-start | bytes 6291464 | tf_op jit(solution)/shard_map/ppermute | solution.py:423
  131.5 28.1 %copy-start.2 = (bf16[8,16,32,128]{3,2,1,0:T(8,128)(2,1)}, bf16[8,16,32,128]{3,2,1,0:T(8,128)(2,1)S(1)}, u32[]{:S(2)}) copy-start(bf16[8,16,32,128]{3,2,1,0:T(8,128)(2,1)S(1)} %all-to-all-done.4.mine_ref) | copy-start | bytes 3145732
  131.5 28.1 %collective-permute-start.5 = (bf16[8,16,32,128]{3,2,1,0:T(8,128)(2,1)S(1)}, bf16[8,16,32,128]{3,2,1,0:T(8,128)(2,1)S(1)}, u32[]{:S(2)}, u32[]{:S(2)}) collective-permute-start(bf16[8,16,32,128]{3,2,1,0:T(8,128)(2,1)S(1)} %all-to-all-done.4.mine_ref), channel_id=1, source_target_pairs={{0,1},{1,0},{2,3},{3,2},{4,5},{5,4},{6,7},{7,6},{8,9},{9,8},{10,11... | collective-permute-start | bytes 3145736 | tf_op jit(solution)/shard_map/ppermute | solution.py:105
  159.7 1.0 copy-start.5
where the time goes:
time: 185 us; the launch traced here: 184 us
  waiting for transfers between devices  65.8 us (36%)
  Pallas kernels  58.9 us (32%)
  starting transfers between devices  25 us (14%)
  blocking collectives  16.9 us (9%)
  local copies, waits for them, and re-layouts  14.9 us (8%)
    all_to_all x1, waiting for transfers between devices, turn(): got = lax.all_to_all(send, 'y', 0, 0, tiled=True)  47 us
    pallas_call x1, Pallas kernels, attend_window(): pl.pallas_call(functools.partial(window_body, n_vert=n_vert, n_slash=n_sl...  26.8 us
    pallas_call x1, Pallas kernels, attend_vertical(): pl.pallas_call(functools.partial(vertical_body, n_vert=n_vert, per_dev=pe...  23.3 us
    all_to_all x1, waiting for transfers between devices, spread_vertical(): lax.all_to_all(jnp.broadcast_to(held, (rows_y, *held.shape)), 'y', 0, 0,...  18.8 us
    all_to_all x1, blocking collectives, turn(): same = lax.all_to_all(send, 'x', 0, 0, tiled=True)  16.9 us
    unnamed x20, local copies, waits for them, and re-layouts  11 us
    pallas_call x3, Pallas kernels, small_call(): pl.pallas_call(body, grid_spec=pltpu.PrefetchScalarGridSpec(num_scalar_pr...  8.83 us
    all_to_all x1, starting transfers between devices, spread_vertical(): lax.all_to_all(jnp.broadcast_to(held, (rows_y, *held.shape)), 'y', 0, 0,...  6.75 us
  transfers between devices with their start and end apart: 7, of which 2 were waited for; matrix products, arithmetic and copies ran while one was open for 5% of the time, Pallas kernels for 18%

commit v1 on v0

--- a/solution.py
+++ b/solution.py
@@ -16,10 +16,21 @@
 ALL = ("y", "x", "core")
 
 
-def shifted(x, by):
-    size = lax.axis_size(ALL)
-    pairs = [(i, i + by) for i in range(size) if 0 <= i + by < size]
-    return lax.ppermute(x, ALL, pairs)
+def hop(x, axis, wrap=False, only=None):
+    size = lax.axis_size(axis)
+    pairs = [(i, (i + 1) % size) for i in range(size) if wrap or i + 1 < size]
+    axes = axis
+    if only is not None:
+        _, index = only
+        axes = ("y", "x")
+        width = lax.axis_size("x")
+        flat = (lambda i: i * width + index) if axis == "y" else (lambda i: index * width + i)
+        pairs = [(flat(i), flat(j)) for i, j in pairs]
+    return lax.ppermute(x, axes, pairs)
+
+
+def from_last_chip(x):
+    return lax.ppermute(x, "x", [(lax.axis_size("x") - 1, 0)])
 
 
 def whole_spec(x):
@@ -114,8 +125,9 @@
         got, rider = lax.optimization_barrier((got, rider))
         send = small_call(functools.partial(keep_body, **static), scalars, (got,), shape_x, [])
         same = lax.all_to_all(send, "x", 0, 0, tiled=True)
+        other = swap(same)
         merged = small_call(
-            functools.partial(merge_body, **static), scalars, (same, swap(same), kept),
+            functools.partial(merge_body, **static), scalars, (same, other, kept),
             kept.shape, [pltpu.SMEM((columns,), jnp.int32)],
         )
         return merged, rider
@@ -141,15 +153,16 @@
 
 def window_body(
     verts, vert_count, slashes, slash_count, place, q_ref, own_ref, core_ref, chip_ref, far_ref,
-    part_ref, stat_ref, keys, vals, lists, *, n_vert, n_slash, per_dev,
+    *rest, n_vert, n_slash, per_dev, skip,
 ):
-    step = pl.program_id(0)
+    part_ref, stat_ref, keys, vals, lists = rest[-5:]
+    step = pl.program_id(0) + skip
     group, _, dim = q_ref.shape[1:]
     scale = math.log2(math.e) / math.sqrt(dim)
     core = place[0] % CORES
     most = n_slash + min(n_vert, per_dev - 1)
 
-    @pl.when(step == 0)
+    @pl.when(step == skip)
     def _():
         fill_ones(vals, dim)
 
@@ -177,99 +190,89 @@
     causal = jnp.concatenate([col <= row] * 2, axis=0)
     lane = col // (dim // group)
 
-    def block(l, carry):
+    def block(item, carry):
+        l, hh = item // PAIR, item % PAIR
         qblock = place[0] * per_dev + l
-        for hh in range(PAIR):
-            head = step * PAIR + hh
-            n_used = vert_count[head]
-            count = jnp.int32(1)
-            for i in range(n_slash):
-                offset = slashes[head * n_slash + i]
-                block_at = qblock - offset
-                ok = (i < slash_count[head]) & (offset > 0) & (block_at >= 0)
-                for j in range(n_vert):
-                    ok = ok & jnp.logical_not((j < n_used) & (verts[head * n_vert + j] == block_at))
-                lists[count] = l - offset + 2 * per_dev
-                count = count + ok.astype(jnp.int32)
+        head = step * PAIR + hh
+        n_used = vert_count[head]
+        count = jnp.int32(1)
+        for i in range(n_slash):
+            offset = slashes[head * n_slash + i]
+            block_at = qblock - offset
+            ok = (i < slash_count[head]) & (offset > 0) & (block_at >= 0)
             for j in range(n_vert):
-                at = verts[head * n_vert + j] - place[0] * per_dev
-                ok = (j < n_used) & (at >= 0) & (at < l)
-                lists[count] = at + 2 * per_dev
-                count = count + ok.astype(jnp.int32)
-
-            def run(n):
-                at = [2 * per_dev + l] + [lists[i] for i in range(1, n)]
-                k = jnp.concatenate([keys[hh, i] for i in at], axis=0)
-                v = jnp.concatenate([vals[hh, i] for i in at], axis=0)
-                rows = pl.ds(l * BLOCK, BLOCK)
-                stat = None
-                for r in range(0, group, 2):
-                    q = q_ref[hh, r : r + 2, rows, :].reshape(2 * BLOCK, dim)
-                    s = lax.dot_general(
-                        q, k, (((1,), (1,)), ((), ())), preferred_element_type=jnp.float32
-                    )
-                    parts = [s[:, i * BLOCK : (i + 1) * BLOCK] for i in range(n)]
-                    parts[0] = jnp.where(causal, parts[0], -jnp.inf)
-                    top = functools.reduce(jnp.maximum, parts)
-                    top = jnp.max(top, axis=-1, keepdims=True) * scale
-                    p = jnp.concatenate(
-                        [jnp.exp2(x * scale - top).astype(jnp.bfloat16) for x in parts], axis=1
-                    )
-                    o = jnp.dot(p, v, preferred_element_type=jnp.float32)
-                    part_ref[hh, r : r + 2, rows, :] = (o[:, :dim] / o[:, dim:]).reshape(
-                        2, BLOCK, dim
-                    )
-                    logs = top + jnp.log2(o[:, dim:])
-                    for i in range(2):
-                        mine = logs[i * BLOCK : (i + 1) * BLOCK]
-                        stat = mine if stat is None else jnp.where(lane == r + i, mine, stat)
-                stat_ref[hh, rows, :] = stat
-
-            for n in range(1, most + 1):
-                pl.when(count == n)(functools.partial(run, n))
+                ok = ok & jnp.logical_not((j < n_used) & (verts[head * n_vert + j] == block_at))
+            lists[count] = l - offset + 2 * per_dev
+            count = count + ok.astype(jnp.int32)
+        for j in range(n_vert):
+            at = verts[head * n_vert + j] - place[0] * per_dev
+            ok = (j < n_used) & (at >= 0) & (at < l)
+            lists[count] = at + 2 * per_dev
+            count = count + ok.astype(jnp.int32)
+
+        def run(n):
+            at = [2 * per_dev + l] + [lists[i] for i in range(1, n)]
+            k = jnp.concatenate([keys[hh, i] for i in at], axis=0)
+            v = jnp.concatenate([vals[hh, i] for i in at], axis=0)
+            rows = pl.ds(l * BLOCK, BLOCK)
+            stat = None
+            for r in range(0, group, 2):
+                q = q_ref[hh, r : r + 2, rows, :].reshape(2 * BLOCK, dim)
+                s = lax.dot_general(
+                    q, k, (((1,), (1,)), ((), ())), preferred_element_type=jnp.float32
+                )
+                parts = [s[:, i * BLOCK : (i + 1) * BLOCK] for i in range(n)]
+                parts[0] = jnp.where(causal, parts[0], -jnp.inf)
+                top = functools.reduce(jnp.maximum, parts)
+                top = jnp.max(top, axis=-1, keepdims=True) * scale
+                p = jnp.concatenate(
+                    [jnp.exp2(x * scale - top).astype(jnp.bfloat16) for x in parts], axis=1
+                )
+                o = jnp.dot(p, v, preferred_element_type=jnp.float32)
+                part_ref[hh, r : r + 2, rows, :] = (o[:, :dim] / o[:, dim:]).reshape(
+                    2, BLOCK, dim
+                )
+                logs = top + jnp.log2(o[:, dim:])
+                for i in range(2):
+                    mine = logs[i * BLOCK : (i + 1) * BLOCK]
+                    stat = mine if stat is None else jnp.where(lane == r + i, mine, stat)
+            stat_ref[hh, rows, :] = stat
+
+        for n in range(1, most + 1):
+            pl.when(count == n)(functools.partial(run, n))
         return carry
 
-    lax.fori_loop(0, per_dev, block, 0)
+    lax.fori_loop(0, per_dev * PAIR, block, 0)
 
 
 def vertical_body(
-    verts, vert_count, place, q_ref, part_ref, stat_ref, mine_ref, theirs_ref, out_ref,
-    keys, vals, wide, s0, s1, p0, p1, t0, t1, *, n_vert, per_dev, half, chunk,
+    verts, vert_count, place, q_ref, part_ref, stat_ref, tiles_ref,
+    *rest, n_vert, per_dev, half, chunk,
 ):
-    step = pl.program_id(0)
+    out_ref, keys, vals, wide, s0, s1, p0, p1, t0, t1 = rest[-10:]
+    step = pl.program_id(0) + place[1] * (half // (PAIR * n_vert))
     group, rows, dim = q_ref.shape[1:]
     scale = math.log2(math.e) / math.sqrt(dim)
-    core = place[0] % CORES
     chunks = rows // chunk
     heads = PAIR * group
 
-    @pl.when(step == 0)
+    @pl.when(pl.program_id(0) == 0)
     def _():
         fill_ones(vals, dim)
 
-    for hh in range(PAIR):
+    def one_head(hh, carry):
         first = (step * PAIR + hh) * n_vert
 
-        def take(source):
-            count = jnp.int32(0)
-            for j in range(n_vert):
-                ok = (j < vert_count[step * PAIR + hh]) & (
-                    verts[first + j] < place[0] * per_dev
-                )
-
-                @pl.when(ok)
-                def _():
-                    tile = source[:, first % half + j].reshape(2 * BLOCK, dim)
-                    keys[hh, count] = tile[:BLOCK]
-                    vals[hh, count, :, :dim] = tile[BLOCK:]
-
-                count = count + ok.astype(jnp.int32)
-
-        pl.when(first // half == core)(lambda: take(mine_ref))
-        pl.when(first // half != core)(lambda: take(theirs_ref))
         count = jnp.int32(0)
         for j in range(n_vert):
             ok = (j < vert_count[step * PAIR + hh]) & (verts[first + j] < place[0] * per_dev)
+
+            @pl.when(ok)
+            def _():
+                tile = tiles_ref[:, first % half + j].reshape(2 * BLOCK, dim)
+                keys[hh, count] = tile[:BLOCK]
+                vals[hh, count, :, :dim] = tile[BLOCK:]
+
             count = count + ok.astype(jnp.int32)
 
         def store(i, r, value):
@@ -325,6 +328,9 @@
 
         for n in range(1, n_vert + 1):
             pl.when(count == n)(functools.partial(run, n))
+        return carry
+
+    lax.fori_loop(0, PAIR, one_head, 0)
 
     def write(i, carry):
         some = wide[pl.ds(i * chunk * heads, chunk * heads), :]
@@ -341,59 +347,74 @@
     )
 
 
-def attend_window(queries, own, core_kv, chip_kv, far, verts, vert_count, slashes, slash_count, device):
+def attend_window(
+    queries, own, core_kv, chip_kv, far, before, verts, vert_count, slashes, slash_count, device,
+    skip,
+):
     heads, group, rows, dim = queries.shape
     per_dev = own.shape[1]
     n_vert = len(verts) // heads
     n_slash = len(slashes) // heads
-    kv_spec = pl.BlockSpec((PAIR, *own.shape[1:]), lambda h, *_: (h, 0, 0, 0))
-    q_spec = pl.BlockSpec((PAIR, group, rows, dim), lambda h, *_: (h, 0, 0, 0))
+    steps = far.shape[0] // PAIR
+    shifted = lambda h, *_: (h + skip, 0, 0, 0)
+    whole_kv = pl.BlockSpec((PAIR, *own.shape[1:]), shifted)
+    half_kv = pl.BlockSpec((PAIR, *own.shape[1:]), lambda h, *_: (h, 0, 0, 0))
+    q_spec = pl.BlockSpec((PAIR, group, rows, dim), shifted)
+    out_shape = [
+        jax.ShapeDtypeStruct(queries.shape, jnp.float32),
+        jax.ShapeDtypeStruct((heads, rows, dim), jnp.float32),
+    ]
     return pl.pallas_call(
-        functools.partial(window_body, n_vert=n_vert, n_slash=n_slash, per_dev=per_dev),
+        functools.partial(
+            window_body, n_vert=n_vert, n_slash=n_slash, per_dev=per_dev, skip=skip
+        ),
         grid_spec=pltpu.PrefetchScalarGridSpec(
             num_scalar_prefetch=5,
-            grid=(heads // PAIR,),
-            in_specs=[q_spec, kv_spec, kv_spec, kv_spec, kv_spec],
-            out_specs=[q_spec, pl.BlockSpec((PAIR, rows, dim), lambda h, *_: (h, 0, 0))],
+            grid=(steps,),
+            in_specs=[q_spec, whole_kv, whole_kv, half_kv, half_kv]
+            + [pl.BlockSpec(memory_space=pl.ANY)] * len(before),
+            out_specs=[q_spec, pl.BlockSpec((PAIR, rows, dim), lambda h, *_: (h + skip, 0, 0))],
             scratch_shapes=[
                 pltpu.VMEM((PAIR, 3 * per_dev, BLOCK, dim), own.dtype),
                 pltpu.VMEM((PAIR, 3 * per_dev, BLOCK, 2 * dim), own.dtype),
                 pltpu.SMEM((n_vert + n_slash + 1,), jnp.int32),
             ],
         ),
-        out_shape=[
-            jax.ShapeDtypeStruct(queries.shape, jnp.float32),
-            jax.ShapeDtypeStruct((heads, rows, dim), jnp.float32),
-        ],
-        cost_estimate=cost(queries, n_slash),
-        name="window",
+        out_shape=out_shape,
+        input_output_aliases={10 + i: i for i in range(len(before))},
+        cost_estimate=cost(queries, n_slash // 2),
     )(
         verts, vert_count, slashes, slash_count, device.reshape(1),
-        queries, own, core_kv, chip_kv, far,
-    )
-
-
-def attend_vertical(queries, part, stat, mine, theirs, verts, vert_count, device, per_dev):
+        queries, own, core_kv, chip_kv, far, *before,
+    )
+
+
+def attend_vertical(queries, part, stat, tiles, before, verts, vert_count, device, which, per_dev):
     heads, group, rows, dim = queries.shape
     n_vert = len(verts) // heads
     chunk = rows // 8
     lines = group * chunk
-    q_spec = pl.BlockSpec((PAIR, group, rows, dim), lambda h, *_: (h, 0, 0, 0))
+    half = tiles.shape[1]
+    steps = half // (PAIR * n_vert)
+    at = lambda h, place: h + place[1] * steps
+    q_spec = pl.BlockSpec((PAIR, group, rows, dim), lambda h, v, c, place: (at(h, place), 0, 0, 0))
     scores = pltpu.VMEM((lines, n_vert * BLOCK), jnp.float32)
     powers = pltpu.VMEM((lines, n_vert * BLOCK), queries.dtype)
     tops = pltpu.VMEM((lines, dim), jnp.float32)
     return pl.pallas_call(
-        functools.partial(
-            vertical_body, n_vert=n_vert, per_dev=per_dev, half=mine.shape[1], chunk=chunk
-        ),
+        functools.partial(vertical_body, n_vert=n_vert, per_dev=per_dev, half=half, chunk=chunk),
         grid_spec=pltpu.PrefetchScalarGridSpec(
             num_scalar_prefetch=3,
-            grid=(heads // PAIR,),
+            grid=(steps,),
             in_specs=[
-                q_spec, q_spec, pl.BlockSpec((PAIR, rows, dim), lambda h, *_: (h, 0, 0)),
-                whole_spec(mine), whole_spec(theirs),
-            ],
-            out_specs=pl.BlockSpec((rows, PAIR * group, dim), lambda h, *_: (0, h, 0)),
+                q_spec, q_spec,
+                pl.BlockSpec((PAIR, rows, dim), lambda h, v, c, place: (at(h, place), 0, 0)),
+                whole_spec(tiles),
+            ]
+            + [pl.BlockSpec(memory_space=pl.ANY)] * len(before),
+            out_specs=pl.BlockSpec(
+                (rows, PAIR * group, dim), lambda h, v, c, place: (0, at(h, place), 0)
+            ),
             scratch_shapes=[
                 pltpu.VMEM((PAIR, n_vert, BLOCK, dim), queries.dtype),
                 pltpu.VMEM((PAIR, n_vert, BLOCK, 2 * dim), queries.dtype),
@@ -402,9 +423,11 @@
             ],
         ),
         out_shape=jax.ShapeDtypeStruct((rows, heads * group, dim), queries.dtype),
-        cost_estimate=cost(queries, n_vert),
-        name="vertical",
-    )(verts, vert_count, device.reshape(1), queries, part, stat, mine, theirs)
+        input_output_aliases={7 + i: i for i in range(len(before))},
+        cost_estimate=cost(queries, n_vert // 2),
+    )(
+        verts, vert_count, jnp.stack((device, which)), queries, part, stat, tiles, *before
+    )
 
 
 def local(
@@ -416,24 +439,35 @@
     per_dev = rows_dev // BLOCK
     n_vert = vert_blocks.shape[1]
     device = lax.axis_index(ALL).astype(jnp.int32)
+    core = device % CORES
     own = jnp.stack((key_states, value_states)).reshape(2, per_dev, BLOCK, kv_heads, head_dim)
     own = jnp.transpose(own, (3, 1, 0, 2, 4)).reshape(kv_heads, per_dev, 2 * BLOCK, head_dim)
-    far = shifted(own, 2)
+    half = kv_heads // 2
+    row_end = lax.axis_size("x") - 1
+    at_start = lax.axis_index("x") == 0
+    low = hop(own[:half], "x", wrap=True)
+    low_wrap = hop(low, "y", only=("x", 0))
+    high = hop(own[half:], "x")
+    high_wrap = hop(own[half:], "y", only=("x", row_end))
+    high_wrap = from_last_chip(high_wrap)
     core_kv = lax.ppermute(own, "core", [(0, 1)])
-    chip_kv = lax.ppermute(far, "core", [(1, 0)])
     verts = vert_blocks.reshape(-1)
+    slashes = slash_offsets.reshape(-1)
     queries = jnp.moveaxis(query_states.reshape(rows_dev, kv_heads, group_size, head_dim), 0, 2)
     mine, theirs, queries = spread_vertical(
         own.reshape(kv_heads * per_dev, 2 * BLOCK, head_dim),
         verts, vert_count, device, per_dev, n_vert, queries,
     )
-    part, stat = attend_window(
-        queries, own, core_kv, chip_kv, far,
-        verts, vert_count, slash_offsets.reshape(-1), slash_count, device,
-    )
-    return attend_vertical(
-        queries, part, stat, mine, theirs, verts, vert_count, device, per_dev
-    )
+    low = jnp.where(at_start, low_wrap, low)
+    high = jnp.where(at_start, high_wrap, high)
+    low_chip = lax.ppermute(low, "core", [(1, 0)])
+    high_chip = lax.ppermute(high, "core", [(1, 0)])
+    lists = (verts, vert_count, slashes, slash_count, device)
+    state = attend_window(queries, own, core_kv, low_chip, low, (), *lists, 0)
+    state = attend_window(queries, own, core_kv, high_chip, high, state, *lists, half // PAIR)
+    lists = (verts, vert_count, device)
+    out = attend_vertical(queries, *state, mine, (), *lists, core, per_dev)
+    return attend_vertical(queries, *state, theirs, (out,), *lists, 1 - core, per_dev)
 
 
 def solution(mesh):

time: 185 us -> 178 us (0.962)
  waiting for transfers between devices: 65.8 us -> 40.5 us
  starting transfers between devices: 25 us -> 48.8 us
  blocking collectives: 16.9 us -> 0 us
  Pallas kernels: 58.9 us -> 66.8 us
  other arithmetic: 1.56 us -> 6.82 us
    all_to_all x1, waiting for transfers between devices: 47 us -> 5.07 us  [turn(): got = lax.all_to_all(send, 'y', 0, 0, tiled=True)]
    ppermute x2 -> x7, waiting for transfers between devices: 0.01 us -> 27 us  [the longest x4 24.6 us: hop(): return lax.ppermute(x, axes, pairs)]
    all_to_all x1, waiting for transfers between devices: 18.8 us -> 0.01 us  [spread_vertical(): lax.all_to_all(jnp.broadcast_to(held, (rows_y, *held.shape)), 'y', 0, 0,...]
    all_to_all x1 -> x0, blocking collectives: 16.9 us -> none  [turn(): same = lax.all_to_all(send, 'x', 0, 0, tiled=True)]
    ppermute x2 -> x7, starting transfers between devices: 9 us -> 24.4 us  [the longest x1 10.3 us: local(): low_chip = lax.ppermute(low, 'core', [(1, 0)])]
    all_to_all x0 -> x1, waiting for transfers between devices: none -> 8.35 us  [turn(): same = lax.all_to_all(send, 'x', 0, 0, tiled=True)]
    all_to_all x0 -> x1, starting transfers between devices: none -> 6.77 us  [turn(): same = lax.all_to_all(send, 'x', 0, 0, tiled=True)]
    select_n x0 -> x2, other arithmetic: none -> 4.62 us  [the longest x1 2.31 us: local(): low = jnp.where(at_start, low_wrap, low)]
  transfers between devices with their start and end apart: 7 -> 13, of which waited for: 2 -> 5; matrix products, arithmetic and copies ran while one was open for 5% -> 9% of each run, Pallas kernels for 18% -> 27%
where the time goes in v1:
time: 178 us
  Pallas kernels  66.8 us (38%)
  starting transfers between devices  48.8 us (27%)
  waiting for transfers between devices  40.5 us (23%)
  local copies, waits for them, and re-layouts  13.8 us (8%)
  other arithmetic  6.82 us (4%)
    pallas_call x2, Pallas kernels, attend_window(): pl.pallas_call(functools.partial(window_body, n_vert=n_vert, n_slash=n_sl...  31 us
    pallas_call x2, Pallas kernels, attend_vertical(): pl.pallas_call(functools.partial(vertical_body, n_vert=n_vert, per_dev=pe...  27.8 us
    ppermute x4, waiting for transfers between devices, hop(): return lax.ppermute(x, axes, pairs)  24.6 us
    ppermute x1, starting transfers between devices, local(): low_chip = lax.ppermute(low, 'core', [(1, 0)])  10.3 us
    unnamed x18, local copies, waits for them, and re-layouts  8.98 us
    all_to_all x1, waiting for transfers between devices, turn(): same = lax.all_to_all(send, 'x', 0, 0, tiled=True)  8.35 us
    pallas_call x3, Pallas kernels, small_call(): pl.pallas_call(body, grid_spec=pltpu.PrefetchScalarGridSpec(num_scalar_pr...  7.98 us
    all_to_all x1, starting transfers between devices, spread_vertical(): lax.all_to_all(jnp.broadcast_to(held, (rows_y, *held.shape)), 'y', 0, 0,...  7.43 us
  transfers between devices with their start and end apart: 13, of which 5 were waited for; matrix products, arithmetic and copies ran while one was open for 9% of the time, Pallas kernels for 27%

profile of v1, /device:TPU:737, one launch (start us, length us, event | category | flops | bytes accessed | tf_op | source)
XLA Modules:
  0.0 177.7 jit_solution(13340247582471374530)
XLA Ops:
  0.0 0.0 copy-start.5
  0.0 0.8 copy.21
  0.8 0.1 reshape.75.verts
  0.9 0.0 copy-start.7
  0.9 1.5 copy_dynamic-update-slice_fusion.1
  2.4 0.0 copy-done.5
  2.4 0.4 copy_dynamic-update-slice_fusion
  2.8 0.7 pad_add_fusion.2.place
  3.5 0.0 copy-done.7
  3.5 2.2 %shard_map.73 = bf16[8,6,32,128]{3,2,1,0:T(8,128)(2,1)} custom-call(s32[32]{0:T(128)S(1)} %reshape.75.verts, s32[8]{0:T(128)S(1)} %copy-done.7, s32[3]{0:T(128)} %pad_add_fusion.2.place, bf16[32,8,32,128]{3,2,1,0:T(8,128)(2,1)S(1)} %bitcast.26), custom_call_target="tpu_custom_call" | custom-call | tf_op jit(solution)/shard_map/pallas_call | solution.py:41
  5.7 5.3 %all-to-all-start.2 = ((bf16[8,6,32,128]{3,2,1,0:T(8,128)(2,1)}), bf16[8,6,32,128]{3,2,1,0:T(8,128)(2,1)S(1)}, u32[]{:S(2)}, u32[]{:S(2)}) async-start(bf16[8,6,32,128]{3,2,1,0:T(8,128)(2,1)} %shard_map.73), calls=%async_computation.2 | async-start | bytes 786432 | tf_op jit(solution)/shard_map/all_to_all | solution.py:124
  10.9 5.8 %copy.24 = bf16[512,32,128]{2,0,1:T(8,128)(2,1)} copy(bf16[512,32,128]{2,1,0:T(8,128)(2,1)} %param.9) | data formatting | bytes 8388608 | tf_op args[0]
  16.7 5.1 %all-to-all-done.2.got = bf16[8,6,32,128]{3,2,1,0:T(8,128)(2,1)S(1)} async-done(((bf16[8,6,32,128]{3,2,1,0:T(8,128)(2,1)}), bf16[8,6,32,128]{3,2,1,0:T(8,128)(2,1)S(1)}, u32[]{:S(2)}, u32[]{:S(2)}) %all-to-all-start.2) | async-done | bytes 393248 | tf_op jit(solution)/shard_map/all_to_all | solution.py:124
  21.8 0.0 copy-start.4
  21.8 0.7 copy-done.4
  22.5 2.8 %shard_map.76 = bf16[8,6,32,128]{3,2,1,0:T(8,128)(2,1)} custom-call(s32[32]{0:T(128)S(1)} %reshape.75.verts, s32[8]{0:T(128)S(1)} %copy-done.7, s32[3]{0:T(128)} %pad_add_fusion.2.place, bf16[8,6,32,128]{3,2,1,0:T(8,128)(2,1)} %copy-done.4), custom_call_target="tpu_custom_call" | custom-call | tf_op jit(solution)/shard_map/pallas_call | solution.py:41
  25.4 6.8 %all-to-all-start.3 = ((bf16[8,6,32,128]{3,2,1,0:T(8,128)(2,1)}), bf16[8,6,32,128]{3,2,1,0:T(8,128)(2,1)S(1)}, u32[]{:S(2)}, u32[]{:S(2)}) async-start(bf16[8,6,32,128]{3,2,1,0:T(8,128)(2,1)} %shard_map.76), calls=%async_computation.3 | async-start | bytes 786432 | tf_op jit(solution)/shard_map/all_to_all | solution.py:127
  32.2 1.6 fusion.2
  33.8 1.5 collective-permute-start.6
  35.2 1.6 collective-permute-start.2
  36.8 8.3 %all-to-all-done.3.same = bf16[8,6,32,128]{3,2,1,0:T(8,128)(2,1)S(1)} async-done(((bf16[8,6,32,128]{3,2,1,0:T(8,128)(2,1)}), bf16[8,6,32,128]{3,2,1,0:T(8,128)(2,1)S(1)}, u32[]{:S(2)}, u32[]{:S(2)}) %all-to-all-start.3) | async-done | bytes 393248 | tf_op jit(solution)/shard_map/all_to_all | solution.py:127
  45.2 0.0 copy-start.3
  45.2 3.7 %collective-permute-start.9 = (bf16[8,6,32,128]{3,2,1,0:T(8,128)(2,1)S(1)}, bf16[8,6,32,128]{3,2,1,0:T(8,128)(2,1)S(1)}, u32[]{:S(2)}, u32[]{:S(2)}) collective-permute-start(bf16[8,6,32,128]{3,2,1,0:T(8,128)(2,1)S(1)} %all-to-all-done.3.same), channel_id=1, source_target_pairs={{0,1},{1,0},{2,3},{3,2},{4,5},{5,4},{6,7},{7,6},{8,9},{9,8},{10,11... | collective-permute-start | bytes 1179656 | tf_op jit(solution)/shard_map/ppermute | solution.py:116
  48.9 0.1 iota_compare_fusion.1
  48.9 0.1 lt.53
  49.0 0.1 convert_reduce_fusion
  49.1 0.7 reduce_max.9
  50.5 15.8 %collective-permute-done.6 = bf16[4,4,256,128]{3,2,1,0:T(8,128)(2,1)} collective-permute-done((bf16[4,4,256,128]{3,2,1,0:T(8,128)(2,1)}, bf16[4,4,256,128]{3,2,1,0:T(8,128)(2,1)}, u32[]{:S(2)}, u32[]{:S(2)}) %collective-permute-start.6) | collective-permute-done | bytes 1048608 | tf_op jit(solution)/shard_map/ppermute | solution.py:29
  66.3 1.9 %collective-permute-start.7 = (bf16[4,4,256,128]{3,2,1,0:T(8,128)(2,1)}, bf16[4,4,256,128]{3,2,1,0:T(8,128)(2,1)}, u32[]{:S(2)}, u32[]{:S(2)}) collective-permute-start(bf16[4,4,256,128]{3,2,1,0:T(8,128)(2,1)} %collective-permute-done.6), channel_id=1, source_target_pairs={{0,16},{16,32},{32,48},{48,64},{64,80},{80,96},{96,112},{1,17},{17... | collective-permute-start | bytes 3145736 | tf_op jit(solution)/shard_map/ppermute | solution.py:29
  68.2 0.0 collective-permute-done.9.other
  68.2 0.0 copy-start.6
  68.3 0.8 broadcast_in_dim.4.old
  69.0 0.0 copy-done.3
  69.0 0.0 copy-done.6
  69.0 2.9 %shard_map.77 = bf16[16,32,128]{2,1,0:T(8,128)(2,1)S(1)} custom-call(s32[32]{0:T(128)S(1)} %reshape.75.verts, s32[8]{0:T(128)S(1)} %copy-done.7, s32[3]{0:T(128)} %pad_add_fusion.2.place, bf16[8,6,32,128]{3,2,1,0:T(8,128)(2,1)} %copy-done.3, bf16[8,6,32,128]{3,2,1,0:T(8,128)(2,1)} %copy-done.6, bf16[16,32,128]{2,1,0:T(8,128)(2,1)} %broadcast_in_dim.4.old), custom_call_target="tpu_custom_call" | custom-call | tf_op jit(solution)/shard_map/pallas_call | solution.py:41
  72.0 0.2 while.14
  72.2 1.2 broadcast_in_dim.5
  73.4 7.4 %all-to-all-start.4 = ((bf16[8,16,32,128]{3,2,1,0:T(8,128)(2,1)}), bf16[8,16,32,128]{3,2,1,0:T(8,128)(2,1)S(1)}, u32[]{:S(2)}, u32[]{:S(2)}) async-start(bf16[8,16,32,128]{3,2,1,0:T(8,128)(2,1)} %broadcast_in_dim.5), calls=%async_computation.4 | async-start | bytes 2097152 | tf_op jit(solution)/shard_map/all_to_all | solution.py:144
  80.8 2.3 %collective-permute-start.4 = (bf16[4,4,256,128]{3,2,1,0:T(8,128)(2,1)}, bf16[4,4,256,128]{3,2,1,0:T(8,128)(2,1)}, u32[]{:S(2)}, u32[]{:S(2)}) collective-permute-start(bf16[4,4,256,128]{3,2,1,0:T(8,128)(2,1)} %bitcast.15), channel_id=1, source_target_pairs={{0,2},{2,4},{4,6},{6,8},{8,10},{10,12},{12,14},{1,3},{3,5},{5,7},{... | collective-permute-start | bytes 3145736 | tf_op jit(solution)/shard_map/ppermute | solution.py:29
  83.1 0.0 collective-permute-done.2
  83.1 1.3 collective-permute-start.3
  84.4 1.3 collective-permute-start.1
  85.7 8.8 %collective-permute-done.7 = bf16[4,4,256,128]{3,2,1,0:T(8,128)(2,1)} collective-permute-done((bf16[4,4,256,128]{3,2,1,0:T(8,128)(2,1)}, bf16[4,4,256,128]{3,2,1,0:T(8,128)(2,1)}, u32[]{:S(2)}, u32[]{:S(2)}) %collective-permute-start.7) | collective-permute-done | bytes 1048608 | tf_op jit(solution)/shard_map/ppermute | solution.py:29
  94.5 2.3 %broadcast_select_fusion.far_ref = bf16[4,4,256,128]{3,2,1,0:T(8,128)(2,1)} fusion(bf16[4,4,256,128]{3,2,1,0:T(8,128)(2,1)} %collective-permute-done.7, bf16[4,4,256,128]{3,2,1,0:T(8,128)(2,1)} %collective-permute-done.6, pred[]{:T(512)S(6)} %eq.25), kind=kLoop, calls=%fused_computation.3 | loop fusion | flops 524288 | bytes 3145729 | tf_op jit(solution)/shard_map/jit(_where)/select_n | solution.py:461
  96.8 10.3 %collective-permute-start.8 = (bf16[4,4,256,128]{3,2,1,0:T(8,128)(2,1)}, bf16[4,4,256,128]{3,2,1,0:T(8,128)(2,1)}, u32[]{:S(2)}, u32[]{:S(2)}) collective-permute-start(bf16[4,4,256,128]{3,2,1,0:T(8,128)(2,1)} %broadcast_select_fusion.far_ref), channel_id=1, source_target_pairs={{1,0},{3,2},{5,4},{7,6},{9,8},{11,10},{13,12},{15,14},{17,16},{19,... | collective-permute-start | bytes 3145736 | tf_op jit(solution)/shard_map/ppermute | solution.py:463
  107.2 0.0 collective-permute-done.4
  107.2 2.4 %collective-permute-done.3 = bf16[4,4,256,128]{3,2,1,0:T(8,128)(2,1)} collective-permute-done((bf16[4,4,256,128]{3,2,1,0:T(8,128)(2,1)}, bf16[4,4,256,128]{3,2,1,0:T(8,128)(2,1)}, u32[]{:S(2)}, u32[]{:S(2)}) %collective-permute-start.3) | collective-permute-done | bytes 1048608 | tf_op jit(solution)/shard_map/ppermute | solution.py:33
  109.6 2.3 %broadcast_select_fusion.1.far_ref = bf16[4,4,256,128]{3,2,1,0:T(8,128)(2,1)} fusion(bf16[4,4,256,128]{3,2,1,0:T(8,128)(2,1)} %collective-permute-done.3, bf16[4,4,256,128]{3,2,1,0:T(8,128)(2,1)} %collective-permute-done.4, pred[]{:T(512)S(6)} %eq.25), kind=kLoop, calls=%fused_computation.4 | loop fusion | flops 524288 | bytes 3145729 | tf_op jit(solution)/shard_map/jit(_where)/select_n | solution.py:462
  111.9 5.4 %collective-permute-start.5 = (bf16[4,4,256,128]{3,2,1,0:T(8,128)(2,1)}, bf16[4,4,256,128]{3,2,1,0:T(8,128)(2,1)}, u32[]{:S(2)}, u32[]{:S(2)}) collective-permute-start(bf16[4,4,256,128]{3,2,1,0:T(8,128)(2,1)} %broadcast_select_fusion.1.far_ref), channel_id=1, source_target_pairs={{1,0},{3,2},{5,4},{7,6},{9,8},{11,10},{13,12},{15,14},{17,16},{19,... | collective-permute-start | bytes 3145736 | tf_op jit(solution)/shard_map/ppermute | solution.py:464
  117.3 0.0 all-to-all-done.4.tiles_ref
  117.3 0.0 collective-permute-start.10
  117.3 0.0 copy-done.8
  117.4 0.1 copy.25
  117.4 0.7 reshape.77.slashes
  118.2 0.7 pad_add_fusion.1
  118.8 0.0 collective-permute-done.1.core_ref
  118.8 0.0 collective-permute-done.8.chip_ref
  118.8 16.4 %shard_map.74 = (f32[8,4,512,128]{3,2,1,0:T(8,128)}, f32[8,512,128]{2,1,0:T(8,128)}) custom-call(s32[32]{0:T(128)S(1)} %get-tuple-element.382, s32[8]{0:T(128)S(1)} %get-tuple-element.383, s32[32]{0:T(128)} %reshape.77.slashes, s32[8]{0:T(128)} %slash_count.3, s32[1]{0:T(128)} %bitcast.3.place, bf16[8,4,512,128]{3,2,1,0:T(8,128)(2,1)} %bitcast.32, ...), custom_call_target="tpu_custom_call" | custom-call | flops 2147483648 | bytes 16777216 | tf_op jit(solution)/shard_map/pallas_call | solution.py:367
  135.2 0.0 copy-done.2
  135.2 0.0 collective-permute-done.5.chip_ref
  135.2 14.6 %shard_map.75 = (f32[8,4,512,128]{3,2,1,0:T(8,128)}, f32[8,512,128]{2,1,0:T(8,128)}) custom-call(s32[32]{0:T(128)S(1)} %get-tuple-element.382, s32[8]{0:T(128)S(1)} %get-tuple-element.383, s32[32]{0:T(128)} %reshape.77.slashes, s32[8]{0:T(128)} %slash_count.3, s32[1]{0:T(128)} %bitcast.3.place, ...), custom_call_target="tpu_custom_call", output_to_operand_aliasing={{0}: (10, {}), {1}: (11, {})} | custom-call | flops 2147483648 | bytes 16777216 | tf_op jit(solution)/shard_map/pallas_call | solution.py:367
  149.9 14.5 %shard_map.78.rest_0_ = bf16[512,32,128]{2,1,0:T(8,128)(2,1)} custom-call(s32[32]{0:T(128)S(1)} %get-tuple-element.382, s32[8]{0:T(128)S(1)} %get-tuple-element.383, s32[2]{0:T(128)} %get-tuple-element.288.place, bf16[8,4,512,128]{3,2,1,0:T(8,128)(2,1)} %bitcast.34, f32[8,4,512,128]{3,2,1,0:T(8,128)} %get-tuple-element.265.part_ref, ...), custom_call_target="tpu_custom_call" | custom-call | flops 2147483648 | bytes 16777216 | tf_op jit(solution)/shard_map/pallas_call | solution.py:404
  164.4 0.0 collective-permute-done.10.tiles_ref
  164.4 13.3 %shard_map.79 = bf16[512,32,128]{2,1,0:T(8,128)(2,1)} custom-call(s32[32]{0:T(128)S(1)} %get-tuple-element.382, s32[8]{0:T(128)S(1)} %get-tuple-element.383, s32[2]{0:T(128)} %get-tuple-element.287.place, bf16[8,4,512,128]{3,2,1,0:T(8,128)(2,1)} %bitcast.35, f32[8,4,512,128]{3,2,1,0:T(8,128)} %get-tuple-element.265.part_ref, ...), custom_call_target="tpu_custom_call", output_to_operand_aliasing={{}: (7, {})} | custom-call | flops 2147483648 | bytes 16777216 | tf_op jit(solution)/shard_map/pallas_call | solution.py:404
  (3 shorter events, 0.0 us)
Async XLA Ops:
  0.0 2.4 %copy-start.5 = (bf16[512,8,128]{2,1,0:T(8,128)(2,1)S(1)}, bf16[512,8,128]{2,1,0:T(8,128)(2,1)}, u32[]{:S(2)}) copy-start(bf16[512,8,128]{2,1,0:T(8,128)(2,1)} %param.11) | copy-start | bytes 3145732
  0.9 2.5 %copy-start.7 = (s32[8]{0:T(128)S(1)}, s32[8]{0:T(128)}, u32[]{:S(2)}) copy-start(s32[8]{0:T(128)} %vert_count.7) | copy-start | bytes 100
  5.7 16.1 %all-to-all-start.2 = ((bf16[8,6,32,128]{3,2,1,0:T(8,128)(2,1)}), bf16[8,6,32,128]{3,2,1,0:T(8,128)(2,1)S(1)}, u32[]{:S(2)}, u32[]{:S(2)}) async-start(bf16[8,6,32,128]{3,2,1,0:T(8,128)(2,1)} %shard_map.73), calls=%async_computation.2 | async-start | bytes 786432 | tf_op jit(solution)/shard_map/all_to_all | solution.py:124
  21.8 0.7 copy-start.4
  25.4 19.8 %all-to-all-start.3 = ((bf16[8,6,32,128]{3,2,1,0:T(8,128)(2,1)}), bf16[8,6,32,128]{3,2,1,0:T(8,128)(2,1)S(1)}, u32[]{:S(2)}, u32[]{:S(2)}) async-start(bf16[8,6,32,128]{3,2,1,0:T(8,128)(2,1)} %shard_map.76), calls=%async_computation.3 | async-start | bytes 786432 | tf_op jit(solution)/shard_map/all_to_all | solution.py:127
  33.8 32.5 %collective-permute-start.6 = (bf16[4,4,256,128]{3,2,1,0:T(8,128)(2,1)}, bf16[4,4,256,128]{3,2,1,0:T(8,128)(2,1)}, u32[]{:S(2)}, u32[]{:S(2)}) collective-permute-start(bf16[4,4,256,128]{3,2,1,0:T(8,128)(2,1)} %bitcast.16), channel_id=1, source_target_pairs={{0,2},{2,4},{4,6},{6,8},{8,10},{10,12},{12,14},{14,0},{1,3},{3,5},... | collective-permute-start | bytes 3145736 | tf_op jit(solution)/shard_map/ppermute | solution.py:29
  35.2 47.9 %collective-permute-start.2 = (bf16[4,4,256,128]{3,2,1,0:T(8,128)(2,1)}, bf16[4,4,256,128]{3,2,1,0:T(8,128)(2,1)}, u32[]{:S(2)}, u32[]{:S(2)}) collective-permute-start(bf16[4,4,256,128]{3,2,1,0:T(8,128)(2,1)} %bitcast.15), channel_id=1, source_target_pairs={{14,30},{30,46},{46,62},{62,78},{78,94},{94,110},{110,126},{15,31}... | collective-permute-start | bytes 3145736 | tf_op jit(solution)/shard_map/ppermute | solution.py:29
  45.2 23.8 %copy-start.3 = (bf16[8,6,32,128]{3,2,1,0:T(8,128)(2,1)}, bf16[8,6,32,128]{3,2,1,0:T(8,128)(2,1)S(1)}, u32[]{:S(2)}) copy-start(bf16[8,6,32,128]{3,2,1,0:T(8,128)(2,1)S(1)} %all-to-all-done.3.same) | copy-start | bytes 1179652
  45.2 23.0 %collective-permute-start.9 = (bf16[8,6,32,128]{3,2,1,0:T(8,128)(2,1)S(1)}, bf16[8,6,32,128]{3,2,1,0:T(8,128)(2,1)S(1)}, u32[]{:S(2)}, u32[]{:S(2)}) collective-permute-start(bf16[8,6,32,128]{3,2,1,0:T(8,128)(2,1)S(1)} %all-to-all-done.3.same), channel_id=1, source_target_pairs={{0,1},{1,0},{2,3},{3,2},{4,5},{5,4},{6,7},{7,6},{8,9},{9,8},{10,11... | collective-permute-start | bytes 1179656 | tf_op jit(solution)/shard_map/ppermute | solution.py:116
  66.3 28.2 %collective-permute-start.7 = (bf16[4,4,256,128]{3,2,1,0:T(8,128)(2,1)}, bf16[4,4,256,128]{3,2,1,0:T(8,128)(2,1)}, u32[]{:S(2)}, u32[]{:S(2)}) collective-permute-start(bf16[4,4,256,128]{3,2,1,0:T(8,128)(2,1)} %collective-permute-done.6), channel_id=1, source_target_pairs={{0,16},{16,32},{32,48},{48,64},{64,80},{80,96},{96,112},{1,17},{17... | collective-permute-start | bytes 3145736 | tf_op jit(solution)/shard_map/ppermute | solution.py:29
  68.2 0.8 copy-start.6
  73.4 44.0 %all-to-all-start.4 = ((bf16[8,16,32,128]{3,2,1,0:T(8,128)(2,1)}), bf16[8,16,32,128]{3,2,1,0:T(8,128)(2,1)S(1)}, u32[]{:S(2)}, u32[]{:S(2)}) async-start(bf16[8,16,32,128]{3,2,1,0:T(8,128)(2,1)} %broadcast_in_dim.5), calls=%async_computation.4 | async-start | bytes 2097152 | tf_op jit(solution)/shard_map/all_to_all | solution.py:144
  80.8 26.4 %collective-permute-start.4 = (bf16[4,4,256,128]{3,2,1,0:T(8,128)(2,1)}, bf16[4,4,256,128]{3,2,1,0:T(8,128)(2,1)}, u32[]{:S(2)}, u32[]{:S(2)}) collective-permute-start(bf16[4,4,256,128]{3,2,1,0:T(8,128)(2,1)} %bitcast.15), channel_id=1, source_target_pairs={{0,2},{2,4},{4,6},{6,8},{8,10},{10,12},{12,14},{1,3},{3,5},{5,7},{... | collective-permute-start | bytes 3145736 | tf_op jit(solution)/shard_map/ppermute | solution.py:29
  83.1 26.5 %collective-permute-start.3 = (bf16[4,4,256,128]{3,2,1,0:T(8,128)(2,1)}, bf16[4,4,256,128]{3,2,1,0:T(8,128)(2,1)}, u32[]{:S(2)}, u32[]{:S(2)}) collective-permute-start(bf16[4,4,256,128]{3,2,1,0:T(8,128)(2,1)} %collective-permute-done.2), channel_id=1, source_target_pairs={{14,0},{15,1},{30,16},{31,17},{46,32},{47,33},{62,48},{63,49},{78,... | collective-permute-start | bytes 3145736 | tf_op jit(solution)/shard_map/ppermute | solution.py:33
  84.4 34.4 %collective-permute-start.1 = (bf16[8,4,256,128]{3,2,1,0:T(8,128)(2,1)S(1)}, bf16[8,4,256,128]{3,2,1,0:T(8,128)(2,1)}, u32[]{:S(2)}, u32[]{:S(2)}) collective-permute-start(bf16[8,4,256,128]{3,2,1,0:T(8,128)(2,1)S(1)} %bitcast.29), channel_id=1, source_target_pairs={{0,1},{2,3},{4,5},{6,7},{8,9},{10,11},{12,13},{14,15},{16,17},{18,... | collective-permute-start | bytes 6291464 | tf_op jit(solution)/shard_map/ppermute | solution.py:453
  96.8 20.5 %copy-start.8 = (s32[8,4]{0,1:T(4,128)S(1)}, s32[8,4]{0,1:T(4,128)}, u32[]{:S(2)}) copy-start(s32[8,4]{0,1:T(4,128)} %param.14) | copy-start | bytes 388
  96.8 22.0 %collective-permute-start.8 = (bf16[4,4,256,128]{3,2,1,0:T(8,128)(2,1)}, bf16[4,4,256,128]{3,2,1,0:T(8,128)(2,1)}, u32[]{:S(2)}, u32[]{:S(2)}) collective-permute-start(bf16[4,4,256,128]{3,2,1,0:T(8,128)(2,1)} %broadcast_select_fusion.far_ref), channel_id=1, source_target_pairs={{1,0},{3,2},{5,4},{7,6},{9,8},{11,10},{13,12},{15,14},{17,16},{19,... | collective-permute-start | bytes 3145736 | tf_op jit(solution)/shard_map/ppermute | solution.py:463
  111.9 23.3 %collective-permute-start.5 = (bf16[4,4,256,128]{3,2,1,0:T(8,128)(2,1)}, bf16[4,4,256,128]{3,2,1,0:T(8,128)(2,1)}, u32[]{:S(2)}, u32[]{:S(2)}) collective-permute-start(bf16[4,4,256,128]{3,2,1,0:T(8,128)(2,1)} %broadcast_select_fusion.1.far_ref), channel_id=1, source_target_pairs={{1,0},{3,2},{5,4},{7,6},{9,8},{11,10},{13,12},{15,14},{17,16},{19,... | collective-permute-start | bytes 3145736 | tf_op jit(solution)/shard_map/ppermute | solution.py:464
  117.3 17.9 %copy-start.2 = (bf16[8,16,32,128]{3,2,1,0:T(8,128)(2,1)}, bf16[8,16,32,128]{3,2,1,0:T(8,128)(2,1)S(1)}, u32[]{:S(2)}) copy-start(bf16[8,16,32,128]{3,2,1,0:T(8,128)(2,1)S(1)} %all-to-all-done.4.tiles_ref) | copy-start | bytes 3145732
  117.3 47.1 %collective-permute-start.10 = (bf16[8,16,32,128]{3,2,1,0:T(8,128)(2,1)S(1)}, bf16[8,16,32,128]{3,2,1,0:T(8,128)(2,1)}, u32[]{:S(2)}, u32[]{:S(2)}) collective-permute-start(bf16[8,16,32,128]{3,2,1,0:T(8,128)(2,1)S(1)} %all-to-all-done.4.tiles_ref), channel_id=1, source_target_pairs={{0,1},{1,0},{2,3},{3,2},{4,5},{5,4},{6,7},{7,6},{8,9},{9,8},{10,11... | collective-permute-start | bytes 3145736 | tf_op jit(solution)/shard_map/ppermute | solution.py:116

commit v2 on v1

--- a/solution.py
+++ b/solution.py
@@ -59,14 +59,16 @@
         yield i, used, owner // columns, owner % columns, (i // n_vert) * per_dev + block % per_dev
 
 
-def pick_body(verts, counts, place, pool, send, *, per_dev, n_vert, columns):
+def pick_body(verts, counts, place, low, high, send, *, per_dev, n_vert, columns):
     seen = jnp.int32(0) - place[2] * SLOTS
-    for _, used, row, col, tile in each_tile(verts, counts, per_dev, n_vert, columns):
+    for i, used, row, col, tile in each_tile(verts, counts, per_dev, n_vert, columns):
         here = used & (col == place[1])
+        first = i // n_vert * per_dev < low.shape[0]
+        pool, base = (low, 0) if first else (high, low.shape[0])
 
         @pl.when(here & (row == place[0]) & (seen >= 0) & (seen < SLOTS))
         def _():
-            send[:, seen] = pool[tile]
+            send[:, seen] = pool[tile - base]
 
         seen = seen + here.astype(jnp.int32)
 
@@ -105,14 +107,14 @@
             out[i % half] = other[col // CORES, slot]
 
 
-def spread_vertical(pool, verts, counts, device, per_dev, n_vert, rider):
+def spread_vertical(low, high, verts, counts, device, per_dev, n_vert, rider):
     rows_y, cols_x = lax.axis_size("y"), lax.axis_size("x")
     columns = cols_x * CORES
-    n_tiles, tile_rows, width = pool.shape
+    tile_rows, width = low.shape[2:]
     piece = tile_rows // rows_y
     half = len(verts) // CORES
     static = dict(per_dev=per_dev, n_vert=n_vert, columns=columns)
-    pool = pool.reshape(n_tiles, rows_y, piece, width)
+    pools = tuple(x.reshape(-1, rows_y, piece, width) for x in (low, high))
     swap = lambda x: lax.ppermute(x, "core", [(0, 1), (1, 0)])
 
     def turn(t, kept, rider):
@@ -120,7 +122,7 @@
         scalars = (verts, counts, place)
         shape_y = (rows_y, SLOTS, piece, width)
         shape_x = (cols_x, SLOTS, piece, width)
-        send = small_call(functools.partial(pick_body, **static), scalars, (pool,), shape_y, [])
+        send = small_call(functools.partial(pick_body, **static), scalars, pools, shape_y, [])
         got = lax.all_to_all(send, "y", 0, 0, tiled=True)
         got, rider = lax.optimization_barrier((got, rider))
         send = small_call(functools.partial(keep_body, **static), scalars, (got,), shape_x, [])
@@ -136,7 +138,7 @@
     column_of = (verts // per_dev) % columns
     load = jnp.sum((column_of[None, :] == jnp.arange(columns)[:, None]) & used, axis=1)
     turns = (jnp.max(load) + SLOTS - 1) // SLOTS
-    first, rider = turn(jnp.int32(0), jnp.zeros((half, piece, width), pool.dtype), rider)
+    first, rider = turn(jnp.int32(0), jnp.zeros((half, piece, width), low.dtype), rider)
     held = lax.while_loop(
         lambda c: c[0] < turns, lambda c: (c[0] + 1, turn(c[0], c[1], ())[0]),
         (jnp.int32(1), first),
@@ -148,25 +150,21 @@
 
 
 def fill_ones(vals, dim):
-    vals[:, :, :, dim:] = jnp.ones((*vals.shape[:3], dim), vals.dtype)
+    vals[..., dim:] = jnp.ones((*vals.shape[:-1], dim), vals.dtype)
 
 
 def window_body(
     verts, vert_count, slashes, slash_count, place, q_ref, own_ref, core_ref, chip_ref, far_ref,
-    *rest, n_vert, n_slash, per_dev, skip,
+    part_ref, stat_ref, keys, vals, lists, *, n_vert, n_slash, per_dev, skip,
 ):
-    part_ref, stat_ref, keys, vals, lists = rest[-5:]
-    step = pl.program_id(0) + skip
     group, _, dim = q_ref.shape[1:]
     scale = math.log2(math.e) / math.sqrt(dim)
     core = place[0] % CORES
     most = n_slash + min(n_vert, per_dev - 1)
 
-    @pl.when(step == skip)
-    def _():
-        fill_ones(vals, dim)
-
-    for hh in range(PAIR):
+    fill_ones(vals, dim)
+
+    def load(hh, carry):
         def put(at, tile):
             keys[hh, at] = tile[:BLOCK]
             vals[hh, at, :, :dim] = tile[BLOCK:]
@@ -184,6 +182,10 @@
         def _():
             for i in range(per_dev):
                 put(per_dev + i, chip_ref[hh, i])
+
+        return carry
+
+    lax.fori_loop(0, part_ref.shape[0], load, 0)
 
     row = lax.broadcasted_iota(jnp.int32, (BLOCK, BLOCK), 0)
     col = lax.broadcasted_iota(jnp.int32, (BLOCK, BLOCK), 1)
@@ -191,9 +193,9 @@
     lane = col // (dim // group)
 
     def block(item, carry):
-        l, hh = item // PAIR, item % PAIR
+        hh, l = item // per_dev, item % per_dev
         qblock = place[0] * per_dev + l
-        head = step * PAIR + hh
+        head = skip + hh
         n_used = vert_count[head]
         count = jnp.int32(1)
         for i in range(n_slash):
@@ -217,7 +219,7 @@
             rows = pl.ds(l * BLOCK, BLOCK)
             stat = None
             for r in range(0, group, 2):
-                q = q_ref[hh, r : r + 2, rows, :].reshape(2 * BLOCK, dim)
+                q = q_ref[head, r : r + 2, rows, :].reshape(2 * BLOCK, dim)
                 s = lax.dot_general(
                     q, k, (((1,), (1,)), ((), ())), preferred_element_type=jnp.float32
                 )
@@ -242,36 +244,36 @@
             pl.when(count == n)(functools.partial(run, n))
         return carry
 
-    lax.fori_loop(0, per_dev * PAIR, block, 0)
+    lax.fori_loop(0, per_dev * part_ref.shape[0], block, 0)
 
 
 def vertical_body(
-    verts, vert_count, place, q_ref, part_ref, stat_ref, tiles_ref,
+    verts, vert_count, place, q_ref, low_part, low_stat, high_part, high_stat, tiles_ref,
     *rest, n_vert, per_dev, half, chunk,
 ):
-    out_ref, keys, vals, wide, s0, s1, p0, p1, t0, t1 = rest[-10:]
-    step = pl.program_id(0) + place[1] * (half // (PAIR * n_vert))
+    out_ref, keys, vals, wide, made, s0, s1, p0, p1, t0, t1, sent = rest[-12:]
+    heads_here = half // n_vert
     group, rows, dim = q_ref.shape[1:]
     scale = math.log2(math.e) / math.sqrt(dim)
     chunks = rows // chunk
     heads = PAIR * group
 
-    @pl.when(pl.program_id(0) == 0)
-    def _():
-        fill_ones(vals, dim)
-
-    def one_head(hh, carry):
-        first = (step * PAIR + hh) * n_vert
+    fill_ones(vals, dim)
+
+    def one_head(at_half, part_ref, stat_ref):
+        hh = at_half % PAIR
+        head = place[1] * heads_here + at_half
+        first = head * n_vert
 
         count = jnp.int32(0)
         for j in range(n_vert):
-            ok = (j < vert_count[step * PAIR + hh]) & (verts[first + j] < place[0] * per_dev)
+            ok = (j < vert_count[head]) & (verts[first + j] < place[0] * per_dev)
 
             @pl.when(ok)
             def _():
                 tile = tiles_ref[:, first % half + j].reshape(2 * BLOCK, dim)
-                keys[hh, count] = tile[:BLOCK]
-                vals[hh, count, :, :dim] = tile[BLOCK:]
+                keys[count] = tile[:BLOCK]
+                vals[count, :, :dim] = tile[BLOCK:]
 
             count = count + ok.astype(jnp.int32)
 
@@ -283,8 +285,8 @@
 
             def stages(i, s_in, s_out, p_in, p_out, t_in, t_out):
                 at = jnp.minimum(i, chunks - 1)
-                q = q_ref[hh, :, pl.ds(at * chunk, chunk), :].reshape(group * chunk, dim)
-                k = keys[hh, :n].reshape(wide_keys, dim)
+                q = q_ref[head, :, pl.ds(at * chunk, chunk), :].reshape(group * chunk, dim)
+                k = keys[:n].reshape(wide_keys, dim)
                 s_in[:, :wide_keys] = lax.dot_general(
                     q, k, (((1,), (1,)), ((), ())), preferred_element_type=jnp.float32
                 ) * scale
@@ -296,9 +298,9 @@
                     )
                 t_in[...] = jnp.broadcast_to(top, t_in.shape)
                 at = jnp.clip(i - 2, 0, chunks - 1)
-                v = vals[hh, :n].reshape(wide_keys, 2 * dim)
+                v = vals[:n].reshape(wide_keys, 2 * dim)
                 o = jnp.dot(p_out[:, :wide_keys], v, preferred_element_type=jnp.float32)
-                stat = stat_ref[hh, pl.ds(at * chunk, chunk), :]
+                stat = stat_ref[at_half, pl.ds(at * chunk, chunk), :]
                 for r in range(group):
                     some = slice(r * chunk, (r + 1) * chunk)
                     lane = r * (dim // group)
@@ -306,7 +308,7 @@
                     new = t_out[some]
                     most = jnp.maximum(logs, new)
                     before, after = jnp.exp2(logs - most), jnp.exp2(new - most)
-                    whole = part_ref[hh, r, pl.ds(at * chunk, chunk), :] * before
+                    whole = part_ref[at_half, r, pl.ds(at * chunk, chunk), :] * before
                     whole = whole + o[some, :dim] * after
                     store(at, r, whole / (before + o[some, dim:] * after))
 
@@ -321,23 +323,44 @@
         def _():
             def copy(i, carry):
                 for r in range(group):
-                    store(i, r, part_ref[hh, r, pl.ds(i * chunk, chunk), :])
+                    store(i, r, part_ref[at_half, r, pl.ds(i * chunk, chunk), :])
                 return carry
 
             lax.fori_loop(0, chunks, copy, 0)
 
         for n in range(1, n_vert + 1):
             pl.when(count == n)(functools.partial(run, n))
+
+    def pair(i, carry):
+        def run_heads(part_ref, stat_ref):
+            def step(hh, carry):
+                one_head(i * PAIR + hh, part_ref, stat_ref)
+                return carry
+
+            lax.fori_loop(0, PAIR, step, 0)
+
+        pl.when(place[1] == 0)(lambda: run_heads(low_part, low_stat))
+        pl.when(place[1] == 1)(lambda: run_heads(high_part, high_stat))
+
+        def write(c, carry):
+            some = wide[pl.ds(c * chunk * heads, chunk * heads), :]
+            made[i, pl.ds(c * chunk, chunk)] = some.reshape(chunk, heads, dim).astype(made.dtype)
+            return carry
+
+        lax.fori_loop(0, chunks, write, 0)
+        send(i).start()
         return carry
 
-    lax.fori_loop(0, PAIR, one_head, 0)
-
-    def write(i, carry):
-        some = wide[pl.ds(i * chunk * heads, chunk * heads), :]
-        out_ref[pl.ds(i * chunk, chunk)] = some.reshape(chunk, heads, dim).astype(out_ref.dtype)
-        return carry
-
-    lax.fori_loop(0, chunks, write, 0)
+    pairs = heads_here // PAIR
+
+    def send(i):
+        at = (place[1] * pairs + i) * heads
+        to = out_ref.at[:, pl.ds(pl.multiple_of(at, heads), heads)]
+        return pltpu.make_async_copy(made.at[i], to, sent.at[i])
+
+    lax.fori_loop(0, pairs, pair, 0)
+    for i in range(pairs):
+        send(i).wait()
 
 
 def cost(queries, tiles):
@@ -347,86 +370,70 @@
     )
 
 
+def in_smem(count):
+    return [pl.BlockSpec(memory_space=pltpu.SMEM)] * count
+
+
+def in_vmem(count):
+    return [pl.BlockSpec(memory_space=pltpu.VMEM)] * count
+
+
 def attend_window(
-    queries, own, core_kv, chip_kv, far, before, verts, vert_count, slashes, slash_count, device,
-    skip,
+    queries, own, core_kv, chip_kv, far, verts, vert_count, slashes, slash_count, device, skip
 ):
     heads, group, rows, dim = queries.shape
-    per_dev = own.shape[1]
+    here, per_dev = own.shape[:2]
     n_vert = len(verts) // heads
     n_slash = len(slashes) // heads
-    steps = far.shape[0] // PAIR
-    shifted = lambda h, *_: (h + skip, 0, 0, 0)
-    whole_kv = pl.BlockSpec((PAIR, *own.shape[1:]), shifted)
-    half_kv = pl.BlockSpec((PAIR, *own.shape[1:]), lambda h, *_: (h, 0, 0, 0))
-    q_spec = pl.BlockSpec((PAIR, group, rows, dim), shifted)
-    out_shape = [
-        jax.ShapeDtypeStruct(queries.shape, jnp.float32),
-        jax.ShapeDtypeStruct((heads, rows, dim), jnp.float32),
-    ]
     return pl.pallas_call(
         functools.partial(
             window_body, n_vert=n_vert, n_slash=n_slash, per_dev=per_dev, skip=skip
         ),
-        grid_spec=pltpu.PrefetchScalarGridSpec(
-            num_scalar_prefetch=5,
-            grid=(steps,),
-            in_specs=[q_spec, whole_kv, whole_kv, half_kv, half_kv]
-            + [pl.BlockSpec(memory_space=pl.ANY)] * len(before),
-            out_specs=[q_spec, pl.BlockSpec((PAIR, rows, dim), lambda h, *_: (h + skip, 0, 0))],
-            scratch_shapes=[
-                pltpu.VMEM((PAIR, 3 * per_dev, BLOCK, dim), own.dtype),
-                pltpu.VMEM((PAIR, 3 * per_dev, BLOCK, 2 * dim), own.dtype),
-                pltpu.SMEM((n_vert + n_slash + 1,), jnp.int32),
-            ],
-        ),
-        out_shape=out_shape,
-        input_output_aliases={10 + i: i for i in range(len(before))},
+        in_specs=in_smem(5) + in_vmem(5),
+        out_specs=in_vmem(2),
+        scratch_shapes=[
+            pltpu.VMEM((here, 3 * per_dev, BLOCK, dim), own.dtype),
+            pltpu.VMEM((here, 3 * per_dev, BLOCK, 2 * dim), own.dtype),
+            pltpu.SMEM((n_vert + n_slash + 1,), jnp.int32),
+        ],
+        out_shape=[
+            jax.ShapeDtypeStruct((here, group, rows, dim), jnp.float32),
+            jax.ShapeDtypeStruct((here, rows, dim), jnp.float32),
+        ],
         cost_estimate=cost(queries, n_slash // 2),
     )(
         verts, vert_count, slashes, slash_count, device.reshape(1),
-        queries, own, core_kv, chip_kv, far, *before,
-    )
-
-
-def attend_vertical(queries, part, stat, tiles, before, verts, vert_count, device, which, per_dev):
+        queries, own, core_kv, chip_kv, far,
+    )
+
+
+def attend_vertical(queries, low, high, tiles, before, verts, vert_count, device, which, per_dev):
     heads, group, rows, dim = queries.shape
     n_vert = len(verts) // heads
     chunk = rows // 8
     lines = group * chunk
     half = tiles.shape[1]
-    steps = half // (PAIR * n_vert)
-    at = lambda h, place: h + place[1] * steps
-    q_spec = pl.BlockSpec((PAIR, group, rows, dim), lambda h, v, c, place: (at(h, place), 0, 0, 0))
+    pairs = half // (PAIR * n_vert)
     scores = pltpu.VMEM((lines, n_vert * BLOCK), jnp.float32)
     powers = pltpu.VMEM((lines, n_vert * BLOCK), queries.dtype)
     tops = pltpu.VMEM((lines, dim), jnp.float32)
     return pl.pallas_call(
         functools.partial(vertical_body, n_vert=n_vert, per_dev=per_dev, half=half, chunk=chunk),
-        grid_spec=pltpu.PrefetchScalarGridSpec(
-            num_scalar_prefetch=3,
-            grid=(steps,),
-            in_specs=[
-                q_spec, q_spec,
-                pl.BlockSpec((PAIR, rows, dim), lambda h, v, c, place: (at(h, place), 0, 0)),
-                whole_spec(tiles),
-            ]
-            + [pl.BlockSpec(memory_space=pl.ANY)] * len(before),
-            out_specs=pl.BlockSpec(
-                (rows, PAIR * group, dim), lambda h, v, c, place: (0, at(h, place), 0)
-            ),
-            scratch_shapes=[
-                pltpu.VMEM((PAIR, n_vert, BLOCK, dim), queries.dtype),
-                pltpu.VMEM((PAIR, n_vert, BLOCK, 2 * dim), queries.dtype),
-                pltpu.VMEM((rows * PAIR * group, dim), jnp.float32),
-                scores, scores, powers, powers, tops, tops,
-            ],
-        ),
+        in_specs=in_smem(3) + in_vmem(6) + [pl.BlockSpec(memory_space=pl.ANY)] * len(before),
+        out_specs=pl.BlockSpec(memory_space=pl.ANY),
+        scratch_shapes=[
+            pltpu.VMEM((n_vert, BLOCK, dim), queries.dtype),
+            pltpu.VMEM((n_vert, BLOCK, 2 * dim), queries.dtype),
+            pltpu.VMEM((rows * PAIR * group, dim), jnp.float32),
+            pltpu.VMEM((pairs, rows, PAIR * group, dim), queries.dtype),
+            scores, scores, powers, powers, tops, tops,
+            pltpu.SemaphoreType.DMA((pairs,)),
+        ],
         out_shape=jax.ShapeDtypeStruct((rows, heads * group, dim), queries.dtype),
-        input_output_aliases={7 + i: i for i in range(len(before))},
+        input_output_aliases={9 + i: i for i in range(len(before))},
         cost_estimate=cost(queries, n_vert // 2),
     )(
-        verts, vert_count, jnp.stack((device, which)), queries, part, stat, tiles, *before
+        verts, vert_count, jnp.stack((device, which)), queries, *low, *high, tiles, *before
     )
 
 
@@ -440,34 +447,39 @@
     n_vert = vert_blocks.shape[1]
     device = lax.axis_index(ALL).astype(jnp.int32)
     core = device % CORES
-    own = jnp.stack((key_states, value_states)).reshape(2, per_dev, BLOCK, kv_heads, head_dim)
-    own = jnp.transpose(own, (3, 1, 0, 2, 4)).reshape(kv_heads, per_dev, 2 * BLOCK, head_dim)
     half = kv_heads // 2
+
+    def pool_of(heads):
+        both = jnp.stack((key_states[:, heads], value_states[:, heads]))
+        both = both.reshape(2, per_dev, BLOCK, half, head_dim)
+        return jnp.transpose(both, (3, 1, 0, 2, 4)).reshape(half, per_dev, 2 * BLOCK, head_dim)
+
+    own_low, own_high = pool_of(slice(0, half)), pool_of(slice(half, None))
     row_end = lax.axis_size("x") - 1
     at_start = lax.axis_index("x") == 0
-    low = hop(own[:half], "x", wrap=True)
+    low = hop(own_low, "x", wrap=True)
     low_wrap = hop(low, "y", only=("x", 0))
-    high = hop(own[half:], "x")
-    high_wrap = hop(own[half:], "y", only=("x", row_end))
+    high = hop(own_high, "x")
+    high_wrap = hop(own_high, "y", only=("x", row_end))
     high_wrap = from_last_chip(high_wrap)
-    core_kv = lax.ppermute(own, "core", [(0, 1)])
+    core_low = lax.ppermute(own_low, "core", [(0, 1)])
+    core_high = lax.ppermute(own_high, "core", [(0, 1)])
     verts = vert_blocks.reshape(-1)
     slashes = slash_offsets.reshape(-1)
     queries = jnp.moveaxis(query_states.reshape(rows_dev, kv_heads, group_size, head_dim), 0, 2)
     mine, theirs, queries = spread_vertical(
-        own.reshape(kv_heads * per_dev, 2 * BLOCK, head_dim),
-        verts, vert_count, device, per_dev, n_vert, queries,
+        own_low, own_high, verts, vert_count, device, per_dev, n_vert, queries,
     )
     low = jnp.where(at_start, low_wrap, low)
     high = jnp.where(at_start, high_wrap, high)
     low_chip = lax.ppermute(low, "core", [(1, 0)])
     high_chip = lax.ppermute(high, "core", [(1, 0)])
     lists = (verts, vert_count, slashes, slash_count, device)
-    state = attend_window(queries, own, core_kv, low_chip, low, (), *lists, 0)
-    state = attend_window(queries, own, core_kv, high_chip, high, state, *lists, half // PAIR)
+    low = attend_window(queries, own_low, core_low, low_chip, low, *lists, 0)
+    high = attend_window(queries, own_high, core_high, high_chip, high, *lists, half)
     lists = (verts, vert_count, device)
-    out = attend_vertical(queries, *state, mine, (), *lists, core, per_dev)
-    return attend_vertical(queries, *state, theirs, (out,), *lists, 1 - core, per_dev)
+    out = attend_vertical(queries, low, high, mine, (), *lists, core, per_dev)
+    return attend_vertical(queries, low, high, theirs, (out,), *lists, 1 - core, per_dev)
 
 
 def solution(mesh):

time: 178 us -> 191 us (1.073)
  the two profiles are of different devices: /device:TPU:737 before, /device:TPU:609 now
where the time goes in v2:
time: 191 us; the launch traced here: 190 us
  Pallas kernels  73.2 us (38%)
  starting transfers between devices  53.8 us (28%)
  waiting for transfers between devices  39.9 us (21%)
  local copies, waits for them, and re-layouts  17.4 us (9%)
  other arithmetic  4.79 us (3%)
    ppermute x4, waiting for transfers between devices, hop(): return lax.ppermute(x, axes, pairs)  33.9 us
    pallas_call x2, Pallas kernels, attend_window(): pl.pallas_call(functools.partial(window_body, n_vert=n_vert, n_slash=n_sl...  33.6 us
    pallas_call x2, Pallas kernels, attend_vertical(): pl.pallas_call(functools.partial(vertical_body, n_vert=n_vert, per_dev=pe...  30.9 us
    all_to_all x1, starting transfers between devices, turn(): same = lax.all_to_all(send, 'x', 0, 0, tiled=True)  10.6 us
    unnamed x27, local copies, waits for them, and re-layouts  10.3 us
    pallas_call x3, Pallas kernels, small_call(): pl.pallas_call(body, grid_spec=pltpu.PrefetchScalarGridSpec(num_scalar_pr...  8.71 us
    ppermute x4, starting transfers between devices, hop(): return lax.ppermute(x, axes, pairs)  8.3 us
    all_to_all x1, starting transfers between devices, spread_vertical(): lax.all_to_all(jnp.broadcast_to(held, (rows_y, *held.shape)), 'y', 0, 0,...  7.38 us
  transfers between devices with their start and end apart: 14, of which 4 were waited for; matrix products, arithmetic and copies ran while one was open for 7% of the time, Pallas kernels for 27%

profile of v2, /device:TPU:609, one launch (start us, length us, event | category | flops | bytes accessed | tf_op | source)
XLA Modules:
  0.0 190.4 jit_solution(10752342257165889814)
XLA Ops:
  0.0 0.8 copy.23
  0.8 0.1 reshape.81.verts
  0.9 2.0 %fusion.3 = (bf16[512,4,128]{2,1,0:T(4,128)(2,1)S(1)}, bf16[512,4,128]{2,1,0:T(4,128)(2,1)S(1)}) fusion(bf16[512,8,128]{2,1,0:T(8,128)(2,1)} %param.10), kind=kLoop, calls=%fused_computation.23 | loop fusion | bytes 2097152 | tf_op jit(solution)/shard_map/slice | solution.py:453
  2.9 0.9 copy_dynamic-update-slice_fusion.3
  3.8 0.9 copy_dynamic-update-slice_fusion.1
  4.7 0.0 copy-done.7
  4.7 0.3 fusion.2
  5.1 0.9 copy_dynamic-update-slice_fusion
  6.0 0.9 copy_dynamic-update-slice_fusion.2
  6.9 0.7 pad_add_fusion.2.place
  7.5 0.0 copy-done.11
  7.5 3.0 %shard_map.73 = bf16[8,6,32,128]{3,2,1,0:T(8,128)(2,1)} custom-call(s32[32]{0:T(128)S(1)} %reshape.81.verts, s32[8]{0:T(128)S(1)} %copy-done.11, s32[3]{0:T(128)} %pad_add_fusion.2.place, bf16[16,8,32,128]{3,2,1,0:T(8,128)(2,1)} %bitcast.10.low, bf16[16,8,32,128]{3,2,1,0:T(8,128)(2,1)} %bitcast.14.high), custom_call_target="tpu_custom_call" | custom-call | tf_op jit(solution)/shard_map/pallas_call | solution.py:41
  10.5 5.3 %all-to-all-start.2 = ((bf16[8,6,32,128]{3,2,1,0:T(8,128)(2,1)}), bf16[8,6,32,128]{3,2,1,0:T(8,128)(2,1)S(1)}, u32[]{:S(2)}, u32[]{:S(2)}) async-start(bf16[8,6,32,128]{3,2,1,0:T(8,128)(2,1)} %shard_map.73), calls=%async_computation.2 | async-start | bytes 786432 | tf_op jit(solution)/shard_map/all_to_all | solution.py:126
  15.8 5.8 %copy.28 = bf16[512,32,128]{2,0,1:T(8,128)(2,1)} copy(bf16[512,32,128]{2,1,0:T(8,128)(2,1)} %param.9) | data formatting | bytes 8388608 | tf_op args[0]
  21.6 1.4 all-to-all-done.2.got
  23.0 0.8 copy-done.6
  23.7 2.8 %shard_map.76 = bf16[8,6,32,128]{3,2,1,0:T(8,128)(2,1)} custom-call(s32[32]{0:T(128)S(1)} %reshape.81.verts, s32[8]{0:T(128)S(1)} %copy-done.11, s32[3]{0:T(128)} %pad_add_fusion.2.place, bf16[8,6,32,128]{3,2,1,0:T(8,128)(2,1)} %copy-done.6), custom_call_target="tpu_custom_call" | custom-call | tf_op jit(solution)/shard_map/pallas_call | solution.py:41
  26.5 10.6 %all-to-all-start.3 = ((bf16[8,6,32,128]{3,2,1,0:T(8,128)(2,1)}), bf16[8,6,32,128]{3,2,1,0:T(8,128)(2,1)S(1)}, u32[]{:S(2)}, u32[]{:S(2)}) async-start(bf16[8,6,32,128]{3,2,1,0:T(8,128)(2,1)} %shard_map.76), calls=%async_computation.3 | async-start | bytes 786432 | tf_op jit(solution)/shard_map/all_to_all | solution.py:129
  37.1 1.7 collective-permute-start.6
  38.8 3.4 %collective-permute-start.8 = (bf16[4,4,256,128]{3,2,1,0:T(8,128)(2,1)}, bf16[4,4,256,128]{3,2,1,0:T(8,128)(2,1)S(1)}, u32[]{:S(2)}, u32[]{:S(2)}) collective-permute-start(bf16[4,4,256,128]{3,2,1,0:T(8,128)(2,1)} %bitcast.19.own_ref), channel_id=1, source_target_pairs={{0,2},{2,4},{4,6},{6,8},{8,10},{10,12},{12,14},{1,3},{3,5},{5,7},{... | collective-permute-start | bytes 3145736 | tf_op jit(solution)/shard_map/ppermute | solution.py:29
  42.3 1.2 collective-permute-start.2
  43.5 4.6 %all-to-all-done.3.same = bf16[8,6,32,128]{3,2,1,0:T(8,128)(2,1)S(1)} async-done(((bf16[8,6,32,128]{3,2,1,0:T(8,128)(2,1)}), bf16[8,6,32,128]{3,2,1,0:T(8,128)(2,1)S(1)}, u32[]{:S(2)}, u32[]{:S(2)}) %all-to-all-start.3) | async-done | bytes 393248 | tf_op jit(solution)/shard_map/all_to_all | solution.py:129
  48.1 7.3 %collective-permute-start.10 = (bf16[8,6,32,128]{3,2,1,0:T(8,128)(2,1)S(1)}, bf16[8,6,32,128]{3,2,1,0:T(8,128)(2,1)S(1)}, u32[]{:S(2)}, u32[]{:S(2)}) collective-permute-start(bf16[8,6,32,128]{3,2,1,0:T(8,128)(2,1)S(1)} %all-to-all-done.3.same), channel_id=1, source_target_pairs={{0,1},{1,0},{2,3},{3,2},{4,5},{5,4},{6,7},{7,6},{8,9},{9,8},{10,11... | collective-permute-start | bytes 1179656 | tf_op jit(solution)/shard_map/ppermute | solution.py:118
  55.3 0.1 iota_compare_fusion.1
  55.4 0.1 lt.53
  55.5 0.1 convert_reduce_fusion
  55.6 0.7 reduce_max.9
  56.9 0.0 collective-permute-done.6
  57.0 1.3 collective-permute-start.7
  58.3 0.0 collective-permute-done.10.other
  58.3 0.7 broadcast_in_dim.4.old
  59.0 0.0 copy-done.10
  59.1 2.9 %shard_map.77 = bf16[16,32,128]{2,1,0:T(8,128)(2,1)S(1)} custom-call(s32[32]{0:T(128)S(1)} %reshape.81.verts, s32[8]{0:T(128)S(1)} %copy-done.11, s32[3]{0:T(128)} %pad_add_fusion.2.place, bf16[8,6,32,128]{3,2,1,0:T(8,128)(2,1)} %copy-done.5, bf16[8,6,32,128]{3,2,1,0:T(8,128)(2,1)} %copy-done.10, bf16[16,32,128]{2,1,0:T(8,128)(2,1)} %broadcast_in_dim.4.old), custom_call_target="tpu_custom_call" | custom-call | tf_op jit(solution)/shard_map/pallas_call | solution.py:41
  62.0 0.2 while.14
  62.2 1.2 broadcast_in_dim.5
  63.4 7.4 %all-to-all-start.4 = ((bf16[8,16,32,128]{3,2,1,0:T(8,128)(2,1)}), bf16[8,16,32,128]{3,2,1,0:T(8,128)(2,1)S(1)}, u32[]{:S(2)}, u32[]{:S(2)}) async-start(bf16[8,16,32,128]{3,2,1,0:T(8,128)(2,1)} %broadcast_in_dim.5), calls=%async_computation.4 | async-start | bytes 2097152 | tf_op jit(solution)/shard_map/all_to_all | solution.py:146
  70.8 19.8 %collective-permute-done.2 = bf16[4,4,256,128]{3,2,1,0:T(8,128)(2,1)S(1)} collective-permute-done((bf16[4,4,256,128]{3,2,1,0:T(8,128)(2,1)}, bf16[4,4,256,128]{3,2,1,0:T(8,128)(2,1)S(1)}, u32[]{:S(2)}, u32[]{:S(2)}) %collective-permute-start.2) | collective-permute-done | bytes 1048608 | tf_op jit(solution)/shard_map/ppermute | solution.py:29
  90.6 1.9 %collective-permute-start.3 = (bf16[4,4,256,128]{3,2,1,0:T(8,128)(2,1)S(1)}, bf16[4,4,256,128]{3,2,1,0:T(8,128)(2,1)}, u32[]{:S(2)}, u32[]{:S(2)}) collective-permute-start(bf16[4,4,256,128]{3,2,1,0:T(8,128)(2,1)S(1)} %collective-permute-done.2), channel_id=1, source_target_pairs={{0,16},{16,32},{32,48},{48,64},{64,80},{80,96},{96,112},{1,17},{17... | collective-permute-start | bytes 3145736 | tf_op jit(solution)/shard_map/ppermute | solution.py:29
  92.5 1.3 collective-permute-start.1
  93.8 1.3 collective-permute-start.5
  95.2 0.0 collective-permute-done.8
  95.2 1.0 copy-done.9
  96.2 0.0 collective-permute-done.7
  96.2 1.3 broadcast_select_fusion.far_ref
  97.5 6.9 %collective-permute-start.9 = (bf16[4,4,256,128]{3,2,1,0:T(8,128)(2,1)S(1)}, bf16[4,4,256,128]{3,2,1,0:T(8,128)(2,1)}, u32[]{:S(2)}, u32[]{:S(2)}) collective-permute-start(bf16[4,4,256,128]{3,2,1,0:T(8,128)(2,1)S(1)} %broadcast_select_fusion.far_ref), channel_id=1, source_target_pairs={{1,0},{3,2},{5,4},{7,6},{9,8},{11,10},{13,12},{15,14},{17,16},{19,... | collective-permute-start | bytes 3145736 | tf_op jit(solution)/shard_map/ppermute | solution.py:476
  104.5 0.0 copy-done.8
  104.5 14.1 %collective-permute-done.3 = bf16[4,4,256,128]{3,2,1,0:T(8,128)(2,1)} collective-permute-done((bf16[4,4,256,128]{3,2,1,0:T(8,128)(2,1)S(1)}, bf16[4,4,256,128]{3,2,1,0:T(8,128)(2,1)}, u32[]{:S(2)}, u32[]{:S(2)}) %collective-permute-start.3) | collective-permute-done | bytes 1048608 | tf_op jit(solution)/shard_map/ppermute | solution.py:29
  118.6 1.3 broadcast_select_fusion.1.far_ref
  119.9 4.2 %collective-permute-start.4 = (bf16[4,4,256,128]{3,2,1,0:T(8,128)(2,1)S(1)}, bf16[4,4,256,128]{3,2,1,0:T(8,128)(2,1)}, u32[]{:S(2)}, u32[]{:S(2)}) collective-permute-start(bf16[4,4,256,128]{3,2,1,0:T(8,128)(2,1)S(1)} %broadcast_select_fusion.1.far_ref), channel_id=1, source_target_pairs={{1,0},{3,2},{5,4},{7,6},{9,8},{11,10},{13,12},{15,14},{17,16},{19,... | collective-permute-start | bytes 3145736 | tf_op jit(solution)/shard_map/ppermute | solution.py:475
  124.1 0.0 all-to-all-done.4.tiles_ref
  124.1 0.0 collective-permute-start.11
  124.1 0.1 copy.29
  124.2 0.9 reshape.83.slashes
  125.1 0.6 pad_add_fusion.1
  125.7 0.0 collective-permute-done.5.core_ref
  125.7 0.0 collective-permute-done.9.chip_ref
  125.7 17.4 %shard_map.75 = (f32[4,4,512,128]{3,2,1,0:T(8,128)}, f32[4,512,128]{2,1,0:T(8,128)}) custom-call(s32[32]{0:T(128)S(1)} %get-tuple-element.410, s32[8]{0:T(128)S(1)} %get-tuple-element.411, s32[32]{0:T(128)} %reshape.83.slashes, s32[8]{0:T(128)} %slash_count.3, s32[1]{0:T(128)} %bitcast.3.place, bf16[8,4,512,128]{3,2,1,0:T(8,128)(2,1)} %bitcast.31, ...), custom_call_target="tpu_custom_call" | custom-call | flops 2147483648 | bytes 16777216 | tf_op jit(solution)/shard_map/pallas_call | solution.py:388
  143.1 0.0 copy-done.3
  143.1 0.0 collective-permute-done.1.core_ref
  143.1 0.0 collective-permute-done.4.chip_ref
  143.1 16.2 %shard_map.74 = (f32[4,4,512,128]{3,2,1,0:T(8,128)}, f32[4,512,128]{2,1,0:T(8,128)}) custom-call(s32[32]{0:T(128)S(1)} %get-tuple-element.410, s32[8]{0:T(128)S(1)} %get-tuple-element.411, s32[32]{0:T(128)} %reshape.83.slashes, s32[8]{0:T(128)} %slash_count.3, s32[1]{0:T(128)} %bitcast.3.place, bf16[8,4,512,128]{3,2,1,0:T(8,128)(2,1)} %bitcast.32, ...), custom_call_target="tpu_custom_call" | custom-call | flops 2147483648 | bytes 16777216 | tf_op jit(solution)/shard_map/pallas_call | solution.py:388
  159.3 15.0 %shard_map.78.rest_0_ = bf16[512,32,128]{2,1,0:T(8,128)(2,1)} custom-call(s32[32]{0:T(128)S(1)} %get-tuple-element.410, s32[8]{0:T(128)S(1)} %get-tuple-element.411, s32[2]{0:T(128)} %get-tuple-element.306.place, bf16[8,4,512,128]{3,2,1,0:T(8,128)(2,1)} %bitcast.33, f32[4,4,512,128]{3,2,1,0:T(8,128)} %get-tuple-element.277.low_part, ...), custom_call_target="tpu_custom_call" | custom-call | flops 2147483648 | bytes 16777216 | tf_op jit(solution)/shard_map/pallas_call | solution.py:420
  174.3 0.0 collective-permute-done.11.tiles_ref
  174.3 15.9 %shard_map.79 = bf16[512,32,128]{2,1,0:T(8,128)(2,1)} custom-call(s32[32]{0:T(128)S(1)} %get-tuple-element.410, s32[8]{0:T(128)S(1)} %get-tuple-element.411, s32[2]{0:T(128)} %get-tuple-element.305.place, bf16[8,4,512,128]{3,2,1,0:T(8,128)(2,1)} %bitcast.34, f32[4,4,512,128]{3,2,1,0:T(8,128)} %get-tuple-element.277.low_part, ...), custom_call_target="tpu_custom_call", output_to_operand_aliasing={{}: (9, {})} | custom-call | flops 2147483648 | bytes 16777216 | tf_op jit(solution)/shard_map/pallas_call | solution.py:420
  (16 shorter events, 0.0 us)
Async XLA Ops:
  0.0 4.7 %copy-start.7 = (bf16[512,8,128]{2,1,0:T(8,128)(2,1)S(1)}, bf16[512,8,128]{2,1,0:T(8,128)(2,1)}, u32[]{:S(2)}) copy-start(bf16[512,8,128]{2,1,0:T(8,128)(2,1)} %param.11) | copy-start | bytes 3145732
  0.9 6.6 %copy-start.11 = (s32[8]{0:T(128)S(1)}, s32[8]{0:T(128)}, u32[]{:S(2)}) copy-start(s32[8]{0:T(128)} %vert_count.7) | copy-start | bytes 100
  10.5 12.5 %all-to-all-start.2 = ((bf16[8,6,32,128]{3,2,1,0:T(8,128)(2,1)}), bf16[8,6,32,128]{3,2,1,0:T(8,128)(2,1)S(1)}, u32[]{:S(2)}, u32[]{:S(2)}) async-start(bf16[8,6,32,128]{3,2,1,0:T(8,128)(2,1)} %shard_map.73), calls=%async_computation.2 | async-start | bytes 786432 | tf_op jit(solution)/shard_map/all_to_all | solution.py:126
  23.0 0.8 copy-start.6
  26.5 21.5 %all-to-all-start.3 = ((bf16[8,6,32,128]{3,2,1,0:T(8,128)(2,1)}), bf16[8,6,32,128]{3,2,1,0:T(8,128)(2,1)S(1)}, u32[]{:S(2)}, u32[]{:S(2)}) async-start(bf16[8,6,32,128]{3,2,1,0:T(8,128)(2,1)} %shard_map.76), calls=%async_computation.3 | async-start | bytes 786432 | tf_op jit(solution)/shard_map/all_to_all | solution.py:129
  37.1 19.8 %collective-permute-start.6 = (bf16[4,4,256,128]{3,2,1,0:T(8,128)(2,1)}, bf16[4,4,256,128]{3,2,1,0:T(8,128)(2,1)}, u32[]{:S(2)}, u32[]{:S(2)}) collective-permute-start(bf16[4,4,256,128]{3,2,1,0:T(8,128)(2,1)} %bitcast.19.own_ref), channel_id=1, source_target_pairs={{14,30},{30,46},{46,62},{62,78},{78,94},{94,110},{110,126},{15,31}... | collective-permute-start | bytes 3145736 | tf_op jit(solution)/shard_map/ppermute | solution.py:29
  38.8 56.4 %collective-permute-start.8 = (bf16[4,4,256,128]{3,2,1,0:T(8,128)(2,1)}, bf16[4,4,256,128]{3,2,1,0:T(8,128)(2,1)S(1)}, u32[]{:S(2)}, u32[]{:S(2)}) collective-permute-start(bf16[4,4,256,128]{3,2,1,0:T(8,128)(2,1)} %bitcast.19.own_ref), channel_id=1, source_target_pairs={{0,2},{2,4},{4,6},{6,8},{8,10},{10,12},{12,14},{1,3},{3,5},{5,7},{... | collective-permute-start | bytes 3145736 | tf_op jit(solution)/shard_map/ppermute | solution.py:29
  42.3 48.3 %collective-permute-start.2 = (bf16[4,4,256,128]{3,2,1,0:T(8,128)(2,1)}, bf16[4,4,256,128]{3,2,1,0:T(8,128)(2,1)S(1)}, u32[]{:S(2)}, u32[]{:S(2)}) collective-permute-start(bf16[4,4,256,128]{3,2,1,0:T(8,128)(2,1)} %bitcast.17.own_ref), channel_id=1, source_target_pairs={{0,2},{2,4},{4,6},{6,8},{8,10},{10,12},{12,14},{14,0},{1,3},{3,5},... | collective-permute-start | bytes 3145736 | tf_op jit(solution)/shard_map/ppermute | solution.py:29
  48.1 11.0 %copy-start.5 = (bf16[8,6,32,128]{3,2,1,0:T(8,128)(2,1)}, bf16[8,6,32,128]{3,2,1,0:T(8,128)(2,1)S(1)}, u32[]{:S(2)}) copy-start(bf16[8,6,32,128]{3,2,1,0:T(8,128)(2,1)S(1)} %all-to-all-done.3.same) | copy-start | bytes 1179652
  48.1 10.2 %collective-permute-start.10 = (bf16[8,6,32,128]{3,2,1,0:T(8,128)(2,1)S(1)}, bf16[8,6,32,128]{3,2,1,0:T(8,128)(2,1)S(1)}, u32[]{:S(2)}, u32[]{:S(2)}) collective-permute-start(bf16[8,6,32,128]{3,2,1,0:T(8,128)(2,1)S(1)} %all-to-all-done.3.same), channel_id=1, source_target_pairs={{0,1},{1,0},{2,3},{3,2},{4,5},{5,4},{6,7},{7,6},{8,9},{9,8},{10,11... | collective-permute-start | bytes 1179656 | tf_op jit(solution)/shard_map/ppermute | solution.py:118
  57.0 39.2 %collective-permute-start.7 = (bf16[4,4,256,128]{3,2,1,0:T(8,128)(2,1)}, bf16[4,4,256,128]{3,2,1,0:T(8,128)(2,1)}, u32[]{:S(2)}, u32[]{:S(2)}) collective-permute-start(bf16[4,4,256,128]{3,2,1,0:T(8,128)(2,1)} %collective-permute-done.6), channel_id=1, source_target_pairs={{14,0},{15,1},{30,16},{31,17},{46,32},{47,33},{62,48},{63,49},{78,... | collective-permute-start | bytes 3145736 | tf_op jit(solution)/shard_map/ppermute | solution.py:33
  58.3 0.8 copy-start.10
  63.4 60.7 %copy-start.12 = (s32[8,4]{0,1:T(4,128)S(1)}, s32[8,4]{0,1:T(4,128)}, u32[]{:S(2)}) copy-start(s32[8,4]{0,1:T(4,128)} %param.14) | copy-start | bytes 388
  63.4 60.7 %all-to-all-start.4 = ((bf16[8,16,32,128]{3,2,1,0:T(8,128)(2,1)}), bf16[8,16,32,128]{3,2,1,0:T(8,128)(2,1)S(1)}, u32[]{:S(2)}, u32[]{:S(2)}) async-start(bf16[8,16,32,128]{3,2,1,0:T(8,128)(2,1)} %broadcast_in_dim.5), calls=%async_computation.4 | async-start | bytes 2097152 | tf_op jit(solution)/shard_map/all_to_all | solution.py:146
  90.6 13.9 %copy-start.8 = (bf16[4,4,256,128]{3,2,1,0:T(8,128)(2,1)}, bf16[4,4,256,128]{3,2,1,0:T(8,128)(2,1)S(1)}, u32[]{:S(2)}) copy-start(bf16[4,4,256,128]{3,2,1,0:T(8,128)(2,1)S(1)} %collective-permute-done.2) | copy-start | bytes 3145732
  90.6 28.0 %collective-permute-start.3 = (bf16[4,4,256,128]{3,2,1,0:T(8,128)(2,1)S(1)}, bf16[4,4,256,128]{3,2,1,0:T(8,128)(2,1)}, u32[]{:S(2)}, u32[]{:S(2)}) collective-permute-start(bf16[4,4,256,128]{3,2,1,0:T(8,128)(2,1)S(1)} %collective-permute-done.2), channel_id=1, source_target_pairs={{0,16},{16,32},{32,48},{48,64},{64,80},{80,96},{96,112},{1,17},{17... | collective-permute-start | bytes 3145736 | tf_op jit(solution)/shard_map/ppermute | solution.py:29
  92.5 50.5 %collective-permute-start.1 = (bf16[4,4,256,128]{3,2,1,0:T(8,128)(2,1)}, bf16[4,4,256,128]{3,2,1,0:T(8,128)(2,1)}, u32[]{:S(2)}, u32[]{:S(2)}) collective-permute-start(bf16[4,4,256,128]{3,2,1,0:T(8,128)(2,1)} %bitcast.17.own_ref), channel_id=1, source_target_pairs={{0,1},{2,3},{4,5},{6,7},{8,9},{10,11},{12,13},{14,15},{16,17},{18,... | collective-permute-start | bytes 3145736 | tf_op jit(solution)/shard_map/ppermute | solution.py:465
  93.8 31.8 %collective-permute-start.5 = (bf16[4,4,256,128]{3,2,1,0:T(8,128)(2,1)}, bf16[4,4,256,128]{3,2,1,0:T(8,128)(2,1)}, u32[]{:S(2)}, u32[]{:S(2)}) collective-permute-start(bf16[4,4,256,128]{3,2,1,0:T(8,128)(2,1)} %bitcast.19.own_ref), channel_id=1, source_target_pairs={{0,1},{2,3},{4,5},{6,7},{8,9},{10,11},{12,13},{14,15},{16,17},{18,... | collective-permute-start | bytes 3145736 | tf_op jit(solution)/shard_map/ppermute | solution.py:466
  95.2 1.0 copy-start.9
  97.5 28.1 %copy-start.4 = (bf16[4,4,256,128]{3,2,1,0:T(8,128)(2,1)}, bf16[4,4,256,128]{3,2,1,0:T(8,128)(2,1)S(1)}, u32[]{:S(2)}) copy-start(bf16[4,4,256,128]{3,2,1,0:T(8,128)(2,1)S(1)} %broadcast_select_fusion.far_ref) | copy-start | bytes 3145732
  97.5 28.1 %collective-permute-start.9 = (bf16[4,4,256,128]{3,2,1,0:T(8,128)(2,1)S(1)}, bf16[4,4,256,128]{3,2,1,0:T(8,128)(2,1)}, u32[]{:S(2)}, u32[]{:S(2)}) collective-permute-start(bf16[4,4,256,128]{3,2,1,0:T(8,128)(2,1)S(1)} %broadcast_select_fusion.far_ref), channel_id=1, source_target_pairs={{1,0},{3,2},{5,4},{7,6},{9,8},{11,10},{13,12},{15,14},{17,16},{19,... | collective-permute-start | bytes 3145736 | tf_op jit(solution)/shard_map/ppermute | solution.py:476
  119.9 23.1 %copy-start.3 = (bf16[4,4,256,128]{3,2,1,0:T(8,128)(2,1)}, bf16[4,4,256,128]{3,2,1,0:T(8,128)(2,1)S(1)}, u32[]{:S(2)}) copy-start(bf16[4,4,256,128]{3,2,1,0:T(8,128)(2,1)S(1)} %broadcast_select_fusion.1.far_ref) | copy-start | bytes 3145732
  119.9 23.2 %collective-permute-start.4 = (bf16[4,4,256,128]{3,2,1,0:T(8,128)(2,1)S(1)}, bf16[4,4,256,128]{3,2,1,0:T(8,128)(2,1)}, u32[]{:S(2)}, u32[]{:S(2)}) collective-permute-start(bf16[4,4,256,128]{3,2,1,0:T(8,128)(2,1)S(1)} %broadcast_select_fusion.1.far_ref), channel_id=1, source_target_pairs={{1,0},{3,2},{5,4},{7,6},{9,8},{11,10},{13,12},{15,14},{17,16},{19,... | collective-permute-start | bytes 3145736 | tf_op jit(solution)/shard_map/ppermute | solution.py:475
  124.1 19.0 %copy-start.2 = (bf16[8,16,32,128]{3,2,1,0:T(8,128)(2,1)}, bf16[8,16,32,128]{3,2,1,0:T(8,128)(2,1)S(1)}, u32[]{:S(2)}) copy-start(bf16[8,16,32,128]{3,2,1,0:T(8,128)(2,1)S(1)} %all-to-all-done.4.tiles_ref) | copy-start | bytes 3145732
  124.1 50.2 %collective-permute-start.11 = (bf16[8,16,32,128]{3,2,1,0:T(8,128)(2,1)S(1)}, bf16[8,16,32,128]{3,2,1,0:T(8,128)(2,1)}, u32[]{:S(2)}, u32[]{:S(2)}) collective-permute-start(bf16[8,16,32,128]{3,2,1,0:T(8,128)(2,1)S(1)} %all-to-all-done.4.tiles_ref), channel_id=1, source_target_pairs={{0,1},{1,0},{2,3},{3,2},{4,5},{5,4},{6,7},{7,6},{8,9},{9,8},{10,11... | collective-permute-start | bytes 3145736 | tf_op jit(solution)/shard_map/ppermute | solution.py:118

commit v3 on v1

--- a/solution.py
+++ b/solution.py
@@ -13,6 +13,7 @@
 SLOTS = 6
 CORES = 2
 PAIR = 2
+WINDOW = 1
 ALL = ("y", "x", "core")
 
 
@@ -148,7 +149,7 @@
 
 
 def fill_ones(vals, dim):
-    vals[:, :, :, dim:] = jnp.ones((*vals.shape[:3], dim), vals.dtype)
+    vals[..., dim:] = jnp.ones((*vals.shape[:-1], dim), vals.dtype)
 
 
 def window_body(
@@ -166,7 +167,7 @@
     def _():
         fill_ones(vals, dim)
 
-    for hh in range(PAIR):
+    for hh in range(WINDOW):
         def put(at, tile):
             keys[hh, at] = tile[:BLOCK]
             vals[hh, at, :, :dim] = tile[BLOCK:]
@@ -191,9 +192,9 @@
     lane = col // (dim // group)
 
     def block(item, carry):
-        l, hh = item // PAIR, item % PAIR
+        l, hh = item // WINDOW, item % WINDOW
         qblock = place[0] * per_dev + l
-        head = step * PAIR + hh
+        head = step * WINDOW + hh
         n_used = vert_count[head]
         count = jnp.int32(1)
         for i in range(n_slash):
@@ -229,8 +230,8 @@
                     [jnp.exp2(x * scale - top).astype(jnp.bfloat16) for x in parts], axis=1
                 )
                 o = jnp.dot(p, v, preferred_element_type=jnp.float32)
-                part_ref[hh, r : r + 2, rows, :] = (o[:, :dim] / o[:, dim:]).reshape(
-                    2, BLOCK, dim
+                part_ref[hh, r : r + 2, rows, :] = (
+                    (o[:, :dim] / o[:, dim:]).astype(part_ref.dtype).reshape(2, BLOCK, dim)
                 )
                 logs = top + jnp.log2(o[:, dim:])
                 for i in range(2):
@@ -242,7 +243,7 @@
             pl.when(count == n)(functools.partial(run, n))
         return carry
 
-    lax.fori_loop(0, per_dev * PAIR, block, 0)
+    lax.fori_loop(0, per_dev * WINDOW, block, 0)
 
 
 def vertical_body(
@@ -250,7 +251,8 @@
     *rest, n_vert, per_dev, half, chunk,
 ):
     out_ref, keys, vals, wide, s0, s1, p0, p1, t0, t1 = rest[-10:]
-    step = pl.program_id(0) + place[1] * (half // (PAIR * n_vert))
+    head = pl.program_id(0) + place[1] * (half // n_vert)
+    hh = head % PAIR
     group, rows, dim = q_ref.shape[1:]
     scale = math.log2(math.e) / math.sqrt(dim)
     chunks = rows // chunk
@@ -260,84 +262,82 @@
     def _():
         fill_ones(vals, dim)
 
-    def one_head(hh, carry):
-        first = (step * PAIR + hh) * n_vert
-
-        count = jnp.int32(0)
-        for j in range(n_vert):
-            ok = (j < vert_count[step * PAIR + hh]) & (verts[first + j] < place[0] * per_dev)
-
-            @pl.when(ok)
-            def _():
-                tile = tiles_ref[:, first % half + j].reshape(2 * BLOCK, dim)
-                keys[hh, count] = tile[:BLOCK]
-                vals[hh, count, :, :dim] = tile[BLOCK:]
-
-            count = count + ok.astype(jnp.int32)
-
-        def store(i, r, value):
-            wide[pl.ds(i * chunk * heads + hh * group + r, chunk, stride=heads), :] = value
-
-        def run(n):
-            wide_keys = n * BLOCK
-
-            def stages(i, s_in, s_out, p_in, p_out, t_in, t_out):
-                at = jnp.minimum(i, chunks - 1)
-                q = q_ref[hh, :, pl.ds(at * chunk, chunk), :].reshape(group * chunk, dim)
-                k = keys[hh, :n].reshape(wide_keys, dim)
-                s_in[:, :wide_keys] = lax.dot_general(
-                    q, k, (((1,), (1,)), ((), ())), preferred_element_type=jnp.float32
-                ) * scale
-                parts = [s_out[:, j * BLOCK : (j + 1) * BLOCK] for j in range(n)]
-                top = jnp.max(functools.reduce(jnp.maximum, parts), axis=-1, keepdims=True)
-                for j in range(n):
-                    p_in[:, j * BLOCK : (j + 1) * BLOCK] = jnp.exp2(parts[j] - top).astype(
-                        jnp.bfloat16
-                    )
-                t_in[...] = jnp.broadcast_to(top, t_in.shape)
-                at = jnp.clip(i - 2, 0, chunks - 1)
-                v = vals[hh, :n].reshape(wide_keys, 2 * dim)
-                o = jnp.dot(p_out[:, :wide_keys], v, preferred_element_type=jnp.float32)
-                stat = stat_ref[hh, pl.ds(at * chunk, chunk), :]
-                for r in range(group):
-                    some = slice(r * chunk, (r + 1) * chunk)
-                    lane = r * (dim // group)
-                    logs = jnp.broadcast_to(stat[:, lane : lane + 1], (chunk, dim))
-                    new = t_out[some]
-                    most = jnp.maximum(logs, new)
-                    before, after = jnp.exp2(logs - most), jnp.exp2(new - most)
-                    whole = part_ref[hh, r, pl.ds(at * chunk, chunk), :] * before
-                    whole = whole + o[some, :dim] * after
-                    store(at, r, whole / (before + o[some, dim:] * after))
-
-            def two(i, carry):
-                stages(2 * i, s0, s1, p1, p0, t1, t0)
-                stages(2 * i + 1, s1, s0, p0, p1, t0, t1)
-                return carry
-
-            lax.fori_loop(0, (chunks + 2) // 2, two, 0)
-
-        @pl.when(count == 0)
-        def _():
-            def copy(i, carry):
-                for r in range(group):
-                    store(i, r, part_ref[hh, r, pl.ds(i * chunk, chunk), :])
-                return carry
-
-            lax.fori_loop(0, chunks, copy, 0)
-
-        for n in range(1, n_vert + 1):
-            pl.when(count == n)(functools.partial(run, n))
-        return carry
-
-    lax.fori_loop(0, PAIR, one_head, 0)
+    first = head * n_vert
+
+    count = jnp.int32(0)
+    for j in range(n_vert):
+        ok = (j < vert_count[head]) & (verts[first + j] < place[0] * per_dev)
+
+        @pl.when(ok)
+        def _():
+            tile = tiles_ref[:, first % half + j].reshape(2 * BLOCK, dim)
+            keys[count] = tile[:BLOCK]
+            vals[count, :, :dim] = tile[BLOCK:]
+
+        count = count + ok.astype(jnp.int32)
+
+    def store(i, r, value):
+        wide[pl.ds(i * chunk * heads + hh * group + r, chunk, stride=heads), :] = value
+
+    def run(n):
+        wide_keys = n * BLOCK
+
+        def stages(i, s_in, s_out, p_in, p_out, t_in, t_out):
+            at = jnp.minimum(i, chunks - 1)
+            q = q_ref[0, :, pl.ds(at * chunk, chunk), :].reshape(group * chunk, dim)
+            k = keys[:n].reshape(wide_keys, dim)
+            s_in[:, :wide_keys] = lax.dot_general(
+                q, k, (((1,), (1,)), ((), ())), preferred_element_type=jnp.float32
+            ) * scale
+            parts = [s_out[:, j * BLOCK : (j + 1) * BLOCK] for j in range(n)]
+            top = jnp.max(functools.reduce(jnp.maximum, parts), axis=-1, keepdims=True)
+            for j in range(n):
+                p_in[:, j * BLOCK : (j + 1) * BLOCK] = jnp.exp2(parts[j] - top).astype(
+                    jnp.bfloat16
+                )
+            t_in[...] = jnp.broadcast_to(top, t_in.shape)
+            at = jnp.clip(i - 2, 0, chunks - 1)
+            v = vals[:n].reshape(wide_keys, 2 * dim)
+            o = jnp.dot(p_out[:, :wide_keys], v, preferred_element_type=jnp.float32)
+            stat = stat_ref[0, pl.ds(at * chunk, chunk), :]
+            for r in range(group):
+                some = slice(r * chunk, (r + 1) * chunk)
+                lane = r * (dim // group)
+                logs = jnp.broadcast_to(stat[:, lane : lane + 1], (chunk, dim))
+                new = t_out[some]
+                most = jnp.maximum(logs, new)
+                before, after = jnp.exp2(logs - most), jnp.exp2(new - most)
+                whole = part_ref[0, r, pl.ds(at * chunk, chunk), :].astype(jnp.float32) * before
+                whole = whole + o[some, :dim] * after
+                store(at, r, whole / (before + o[some, dim:] * after))
+
+        def two(i, carry):
+            stages(2 * i, s0, s1, p1, p0, t1, t0)
+            stages(2 * i + 1, s1, s0, p0, p1, t0, t1)
+            return carry
+
+        lax.fori_loop(0, (chunks + 2) // 2, two, 0)
+
+    @pl.when(count == 0)
+    def _():
+        def copy(i, carry):
+            for r in range(group):
+                store(i, r, part_ref[0, r, pl.ds(i * chunk, chunk), :].astype(jnp.float32))
+            return carry
+
+        lax.fori_loop(0, chunks, copy, 0)
+
+    for n in range(1, n_vert + 1):
+        pl.when(count == n)(functools.partial(run, n))
 
     def write(i, carry):
         some = wide[pl.ds(i * chunk * heads, chunk * heads), :]
         out_ref[pl.ds(i * chunk, chunk)] = some.reshape(chunk, heads, dim).astype(out_ref.dtype)
         return carry
 
-    lax.fori_loop(0, chunks, write, 0)
+    @pl.when(hh == PAIR - 1)
+    def _():
+        lax.fori_loop(0, chunks, write, 0)
 
 
 def cost(queries, tiles):
@@ -355,13 +355,13 @@
     per_dev = own.shape[1]
     n_vert = len(verts) // heads
     n_slash = len(slashes) // heads
-    steps = far.shape[0] // PAIR
+    steps = far.shape[0] // WINDOW
     shifted = lambda h, *_: (h + skip, 0, 0, 0)
-    whole_kv = pl.BlockSpec((PAIR, *own.shape[1:]), shifted)
-    half_kv = pl.BlockSpec((PAIR, *own.shape[1:]), lambda h, *_: (h, 0, 0, 0))
-    q_spec = pl.BlockSpec((PAIR, group, rows, dim), shifted)
+    whole_kv = pl.BlockSpec((WINDOW, *own.shape[1:]), shifted)
+    half_kv = pl.BlockSpec((WINDOW, *own.shape[1:]), lambda h, *_: (h, 0, 0, 0))
+    q_spec = pl.BlockSpec((WINDOW, group, rows, dim), shifted)
     out_shape = [
-        jax.ShapeDtypeStruct(queries.shape, jnp.float32),
+        jax.ShapeDtypeStruct(queries.shape, queries.dtype),
         jax.ShapeDtypeStruct((heads, rows, dim), jnp.float32),
     ]
     return pl.pallas_call(
@@ -373,10 +373,10 @@
             grid=(steps,),
             in_specs=[q_spec, whole_kv, whole_kv, half_kv, half_kv]
             + [pl.BlockSpec(memory_space=pl.ANY)] * len(before),
-            out_specs=[q_spec, pl.BlockSpec((PAIR, rows, dim), lambda h, *_: (h + skip, 0, 0))],
+            out_specs=[q_spec, pl.BlockSpec((WINDOW, rows, dim), lambda h, *_: (h + skip, 0, 0))],
             scratch_shapes=[
-                pltpu.VMEM((PAIR, 3 * per_dev, BLOCK, dim), own.dtype),
-                pltpu.VMEM((PAIR, 3 * per_dev, BLOCK, 2 * dim), own.dtype),
+                pltpu.VMEM((WINDOW, 3 * per_dev, BLOCK, dim), own.dtype),
+                pltpu.VMEM((WINDOW, 3 * per_dev, BLOCK, 2 * dim), own.dtype),
                 pltpu.SMEM((n_vert + n_slash + 1,), jnp.int32),
             ],
         ),
@@ -395,9 +395,9 @@
     chunk = rows // 8
     lines = group * chunk
     half = tiles.shape[1]
-    steps = half // (PAIR * n_vert)
+    steps = half // n_vert
     at = lambda h, place: h + place[1] * steps
-    q_spec = pl.BlockSpec((PAIR, group, rows, dim), lambda h, v, c, place: (at(h, place), 0, 0, 0))
+    q_spec = pl.BlockSpec((1, group, rows, dim), lambda h, v, c, place: (at(h, place), 0, 0, 0))
     scores = pltpu.VMEM((lines, n_vert * BLOCK), jnp.float32)
     powers = pltpu.VMEM((lines, n_vert * BLOCK), queries.dtype)
     tops = pltpu.VMEM((lines, dim), jnp.float32)
@@ -408,16 +408,16 @@
             grid=(steps,),
             in_specs=[
                 q_spec, q_spec,
-                pl.BlockSpec((PAIR, rows, dim), lambda h, v, c, place: (at(h, place), 0, 0)),
+                pl.BlockSpec((1, rows, dim), lambda h, v, c, place: (at(h, place), 0, 0)),
                 whole_spec(tiles),
             ]
             + [pl.BlockSpec(memory_space=pl.ANY)] * len(before),
             out_specs=pl.BlockSpec(
-                (rows, PAIR * group, dim), lambda h, v, c, place: (0, at(h, place), 0)
+                (rows, PAIR * group, dim), lambda h, v, c, place: (0, at(h, place) // PAIR, 0)
             ),
             scratch_shapes=[
-                pltpu.VMEM((PAIR, n_vert, BLOCK, dim), queries.dtype),
-                pltpu.VMEM((PAIR, n_vert, BLOCK, 2 * dim), queries.dtype),
+                pltpu.VMEM((n_vert, BLOCK, dim), queries.dtype),
+                pltpu.VMEM((n_vert, BLOCK, 2 * dim), queries.dtype),
                 pltpu.VMEM((rows * PAIR * group, dim), jnp.float32),
                 scores, scores, powers, powers, tops, tops,
             ],
@@ -464,7 +464,7 @@
     high_chip = lax.ppermute(high, "core", [(1, 0)])
     lists = (verts, vert_count, slashes, slash_count, device)
     state = attend_window(queries, own, core_kv, low_chip, low, (), *lists, 0)
-    state = attend_window(queries, own, core_kv, high_chip, high, state, *lists, half // PAIR)
+    state = attend_window(queries, own, core_kv, high_chip, high, state, *lists, half // WINDOW)
     lists = (verts, vert_count, device)
     out = attend_vertical(queries, *state, mine, (), *lists, core, per_dev)
     return attend_vertical(queries, *state, theirs, (out,), *lists, 1 - core, per_dev)

time: 178 us -> 174 us (0.978)
  the two profiles are of different devices: /device:TPU:737 before, /device:TPU:705 now
where the time goes in v3:
time: 174 us; the launch traced here: 173 us
  Pallas kernels  59.9 us (34%)
  starting transfers between devices  58.6 us (34%)
  waiting for transfers between devices  33.4 us (19%)
  local copies, waits for them, and re-layouts  13.8 us (8%)
  other arithmetic  6.81 us (4%)
    pallas_call x2, Pallas kernels, attend_window(): pl.pallas_call(functools.partial(window_body, n_vert=n_vert, n_slash=n_sl...  28.9 us
    pallas_call x2, Pallas kernels, attend_vertical(): pl.pallas_call(functools.partial(vertical_body, n_vert=n_vert, per_dev=pe...  23 us
    ppermute x4, waiting for transfers between devices, hop(): return lax.ppermute(x, axes, pairs)  19.1 us
    ppermute x1, starting transfers between devices, local(): low_chip = lax.ppermute(low, 'core', [(1, 0)])  13.2 us
    all_to_all x1, starting transfers between devices, spread_vertical(): lax.all_to_all(jnp.broadcast_to(held, (rows_y, *held.shape)), 'y', 0, 0,...  10.2 us
    unnamed x18, local copies, waits for them, and re-layouts  8.94 us
    pallas_call x3, Pallas kernels, small_call(): pl.pallas_call(body, grid_spec=pltpu.PrefetchScalarGridSpec(num_scalar_pr...  7.98 us
    all_to_all x1, starting transfers between devices, turn(): got = lax.all_to_all(send, 'y', 0, 0, tiled=True)  7.91 us
  transfers between devices with their start and end apart: 13, of which 5 were waited for; matrix products, arithmetic and copies ran while one was open for 9% of the time, Pallas kernels for 25%

profile of v3, /device:TPU:705, one launch (start us, length us, event | category | flops | bytes accessed | tf_op | source)
XLA Modules:
  0.0 173.5 jit_solution(5699649911405639782)
XLA Ops:
  0.0 0.8 copy.21
  0.8 0.1 reshape.75.verts
  0.9 0.0 copy-start.7
  0.9 1.5 copy_dynamic-update-slice_fusion.1
  2.4 0.0 copy-done.5
  2.4 0.4 copy_dynamic-update-slice_fusion
  2.8 0.7 pad_add_fusion.2.place
  3.5 0.0 copy-done.7
  3.5 2.2 %shard_map.73 = bf16[8,6,32,128]{3,2,1,0:T(8,128)(2,1)} custom-call(s32[32]{0:T(128)S(1)} %reshape.75.verts, s32[8]{0:T(128)S(1)} %copy-done.7, s32[3]{0:T(128)} %pad_add_fusion.2.place, bf16[32,8,32,128]{3,2,1,0:T(8,128)(2,1)S(1)} %bitcast.26), custom_call_target="tpu_custom_call" | custom-call | tf_op jit(solution)/shard_map/pallas_call | solution.py:42
  5.7 7.9 %all-to-all-start.2 = ((bf16[8,6,32,128]{3,2,1,0:T(8,128)(2,1)}), bf16[8,6,32,128]{3,2,1,0:T(8,128)(2,1)S(1)}, u32[]{:S(2)}, u32[]{:S(2)}) async-start(bf16[8,6,32,128]{3,2,1,0:T(8,128)(2,1)} %shard_map.73), calls=%async_computation.2 | async-start | bytes 786432 | tf_op jit(solution)/shard_map/all_to_all | solution.py:125
  13.6 5.7 %copy.24 = bf16[512,32,128]{2,0,1:T(8,128)(2,1)} copy(bf16[512,32,128]{2,1,0:T(8,128)(2,1)} %param.9) | data formatting | bytes 8388608 | tf_op args[0]
  19.3 2.8 %all-to-all-done.2.got = bf16[8,6,32,128]{3,2,1,0:T(8,128)(2,1)S(1)} async-done(((bf16[8,6,32,128]{3,2,1,0:T(8,128)(2,1)}), bf16[8,6,32,128]{3,2,1,0:T(8,128)(2,1)S(1)}, u32[]{:S(2)}, u32[]{:S(2)}) %all-to-all-start.2) | async-done | bytes 393248 | tf_op jit(solution)/shard_map/all_to_all | solution.py:125
  22.1 0.0 copy-start.4
  22.1 0.7 copy-done.4
  22.9 2.9 %shard_map.76 = bf16[8,6,32,128]{3,2,1,0:T(8,128)(2,1)} custom-call(s32[32]{0:T(128)S(1)} %reshape.75.verts, s32[8]{0:T(128)S(1)} %copy-done.7, s32[3]{0:T(128)} %pad_add_fusion.2.place, bf16[8,6,32,128]{3,2,1,0:T(8,128)(2,1)} %copy-done.4), custom_call_target="tpu_custom_call" | custom-call | tf_op jit(solution)/shard_map/pallas_call | solution.py:42
  25.7 6.8 %all-to-all-start.3 = ((bf16[8,6,32,128]{3,2,1,0:T(8,128)(2,1)}), bf16[8,6,32,128]{3,2,1,0:T(8,128)(2,1)S(1)}, u32[]{:S(2)}, u32[]{:S(2)}) async-start(bf16[8,6,32,128]{3,2,1,0:T(8,128)(2,1)} %shard_map.76), calls=%async_computation.3 | async-start | bytes 786432 | tf_op jit(solution)/shard_map/all_to_all | solution.py:128
  32.5 1.6 fusion.2
  34.1 1.5 collective-permute-start.6
  35.6 1.6 collective-permute-start.2
  37.2 7.3 %all-to-all-done.3.same = bf16[8,6,32,128]{3,2,1,0:T(8,128)(2,1)S(1)} async-done(((bf16[8,6,32,128]{3,2,1,0:T(8,128)(2,1)}), bf16[8,6,32,128]{3,2,1,0:T(8,128)(2,1)S(1)}, u32[]{:S(2)}, u32[]{:S(2)}) %all-to-all-start.3) | async-done | bytes 393248 | tf_op jit(solution)/shard_map/all_to_all | solution.py:128
  44.5 0.0 copy-start.3
  44.5 5.2 %collective-permute-start.9 = (bf16[8,6,32,128]{3,2,1,0:T(8,128)(2,1)S(1)}, bf16[8,6,32,128]{3,2,1,0:T(8,128)(2,1)S(1)}, u32[]{:S(2)}, u32[]{:S(2)}) collective-permute-start(bf16[8,6,32,128]{3,2,1,0:T(8,128)(2,1)S(1)} %all-to-all-done.3.same), channel_id=1, source_target_pairs={{0,1},{1,0},{2,3},{3,2},{4,5},{5,4},{6,7},{7,6},{8,9},{9,8},{10,11... | collective-permute-start | bytes 1179656 | tf_op jit(solution)/shard_map/ppermute | solution.py:117
  49.7 0.1 iota_compare_fusion.1
  49.8 0.1 lt.53
  49.9 0.1 convert_reduce_fusion
  50.0 0.7 reduce_max.9
  51.4 14.8 %collective-permute-done.6 = bf16[4,4,256,128]{3,2,1,0:T(8,128)(2,1)} collective-permute-done((bf16[4,4,256,128]{3,2,1,0:T(8,128)(2,1)}, bf16[4,4,256,128]{3,2,1,0:T(8,128)(2,1)}, u32[]{:S(2)}, u32[]{:S(2)}) %collective-permute-start.6) | collective-permute-done | bytes 1048608 | tf_op jit(solution)/shard_map/ppermute | solution.py:30
  66.2 1.9 %collective-permute-start.7 = (bf16[4,4,256,128]{3,2,1,0:T(8,128)(2,1)}, bf16[4,4,256,128]{3,2,1,0:T(8,128)(2,1)}, u32[]{:S(2)}, u32[]{:S(2)}) collective-permute-start(bf16[4,4,256,128]{3,2,1,0:T(8,128)(2,1)} %collective-permute-done.6), channel_id=1, source_target_pairs={{0,16},{16,32},{32,48},{48,64},{64,80},{80,96},{96,112},{1,17},{17... | collective-permute-start | bytes 3145736 | tf_op jit(solution)/shard_map/ppermute | solution.py:30
  68.2 0.0 collective-permute-done.9.other
  68.2 0.0 copy-start.6
  68.2 0.7 broadcast_in_dim.4.old
  69.0 0.0 copy-done.3
  69.0 0.0 copy-done.6
  69.0 2.9 %shard_map.77 = bf16[16,32,128]{2,1,0:T(8,128)(2,1)S(1)} custom-call(s32[32]{0:T(128)S(1)} %reshape.75.verts, s32[8]{0:T(128)S(1)} %copy-done.7, s32[3]{0:T(128)} %pad_add_fusion.2.place, bf16[8,6,32,128]{3,2,1,0:T(8,128)(2,1)} %copy-done.3, bf16[8,6,32,128]{3,2,1,0:T(8,128)(2,1)} %copy-done.6, bf16[16,32,128]{2,1,0:T(8,128)(2,1)} %broadcast_in_dim.4.old), custom_call_target="tpu_custom_call" | custom-call | tf_op jit(solution)/shard_map/pallas_call | solution.py:42
  71.9 0.2 while.14
  72.1 1.2 broadcast_in_dim.5
  73.3 10.2 %all-to-all-start.4 = ((bf16[8,16,32,128]{3,2,1,0:T(8,128)(2,1)}), bf16[8,16,32,128]{3,2,1,0:T(8,128)(2,1)S(1)}, u32[]{:S(2)}, u32[]{:S(2)}) async-start(bf16[8,16,32,128]{3,2,1,0:T(8,128)(2,1)} %broadcast_in_dim.5), calls=%async_computation.4 | async-start | bytes 2097152 | tf_op jit(solution)/shard_map/all_to_all | solution.py:145
  83.5 2.3 %collective-permute-start.4 = (bf16[4,4,256,128]{3,2,1,0:T(8,128)(2,1)}, bf16[4,4,256,128]{3,2,1,0:T(8,128)(2,1)}, u32[]{:S(2)}, u32[]{:S(2)}) collective-permute-start(bf16[4,4,256,128]{3,2,1,0:T(8,128)(2,1)} %bitcast.15), channel_id=1, source_target_pairs={{0,2},{2,4},{4,6},{6,8},{8,10},{10,12},{12,14},{1,3},{3,5},{5,7},{... | collective-permute-start | bytes 3145736 | tf_op jit(solution)/shard_map/ppermute | solution.py:30
  85.8 0.0 collective-permute-done.2
  85.8 1.3 collective-permute-start.3
  87.1 1.3 collective-permute-start.1
  88.4 4.2 %collective-permute-done.7 = bf16[4,4,256,128]{3,2,1,0:T(8,128)(2,1)} collective-permute-done((bf16[4,4,256,128]{3,2,1,0:T(8,128)(2,1)}, bf16[4,4,256,128]{3,2,1,0:T(8,128)(2,1)}, u32[]{:S(2)}, u32[]{:S(2)}) %collective-permute-start.7) | collective-permute-done | bytes 1048608 | tf_op jit(solution)/shard_map/ppermute | solution.py:30
  92.6 2.3 %broadcast_select_fusion.far_ref = bf16[4,4,256,128]{3,2,1,0:T(8,128)(2,1)} fusion(bf16[4,4,256,128]{3,2,1,0:T(8,128)(2,1)} %collective-permute-done.7, bf16[4,4,256,128]{3,2,1,0:T(8,128)(2,1)} %collective-permute-done.6, pred[]{:T(512)S(6)} %eq.25), kind=kLoop, calls=%fused_computation.3 | loop fusion | flops 524288 | bytes 3145729 | tf_op jit(solution)/shard_map/jit(_where)/select_n | solution.py:461
  94.9 0.0 copy-start.8
  94.9 13.2 %collective-permute-start.8 = (bf16[4,4,256,128]{3,2,1,0:T(8,128)(2,1)}, bf16[4,4,256,128]{3,2,1,0:T(8,128)(2,1)}, u32[]{:S(2)}, u32[]{:S(2)}) collective-permute-start(bf16[4,4,256,128]{3,2,1,0:T(8,128)(2,1)} %broadcast_select_fusion.far_ref), channel_id=1, source_target_pairs={{1,0},{3,2},{5,4},{7,6},{9,8},{11,10},{13,12},{15,14},{17,16},{19,... | collective-permute-start | bytes 3145736 | tf_op jit(solution)/shard_map/ppermute | solution.py:463
  108.1 0.0 collective-permute-done.4
  108.1 4.2 %collective-permute-done.3 = bf16[4,4,256,128]{3,2,1,0:T(8,128)(2,1)} collective-permute-done((bf16[4,4,256,128]{3,2,1,0:T(8,128)(2,1)}, bf16[4,4,256,128]{3,2,1,0:T(8,128)(2,1)}, u32[]{:S(2)}, u32[]{:S(2)}) %collective-permute-start.3) | collective-permute-done | bytes 1048608 | tf_op jit(solution)/shard_map/ppermute | solution.py:34
  112.3 2.3 %broadcast_select_fusion.1.far_ref = bf16[4,4,256,128]{3,2,1,0:T(8,128)(2,1)} fusion(bf16[4,4,256,128]{3,2,1,0:T(8,128)(2,1)} %collective-permute-done.3, bf16[4,4,256,128]{3,2,1,0:T(8,128)(2,1)} %collective-permute-done.4, pred[]{:T(512)S(6)} %eq.25), kind=kLoop, calls=%fused_computation.4 | loop fusion | flops 524288 | bytes 3145729 | tf_op jit(solution)/shard_map/jit(_where)/select_n | solution.py:462
  114.6 5.4 %collective-permute-start.5 = (bf16[4,4,256,128]{3,2,1,0:T(8,128)(2,1)}, bf16[4,4,256,128]{3,2,1,0:T(8,128)(2,1)}, u32[]{:S(2)}, u32[]{:S(2)}) collective-permute-start(bf16[4,4,256,128]{3,2,1,0:T(8,128)(2,1)} %broadcast_select_fusion.1.far_ref), channel_id=1, source_target_pairs={{1,0},{3,2},{5,4},{7,6},{9,8},{11,10},{13,12},{15,14},{17,16},{19,... | collective-permute-start | bytes 3145736 | tf_op jit(solution)/shard_map/ppermute | solution.py:464
  120.0 0.0 all-to-all-done.4.tiles_ref
  120.0 0.0 collective-permute-start.10
  120.0 0.0 copy-done.8
  120.0 0.1 copy.25
  120.1 0.8 reshape.77.slashes
  120.9 0.6 pad_add_fusion.1
  121.5 0.0 collective-permute-done.1.core_ref
  121.5 0.0 collective-permute-done.8.chip_ref
  121.5 15.3 %shard_map.74 = (bf16[8,4,512,128]{3,2,1,0:T(8,128)(2,1)}, f32[8,512,128]{2,1,0:T(8,128)}) custom-call(s32[32]{0:T(128)S(1)} %get-tuple-element.382, s32[8]{0:T(128)S(1)} %get-tuple-element.383, s32[32]{0:T(128)} %reshape.77.slashes, s32[8]{0:T(128)} %slash_count.3, s32[1]{0:T(128)} %bitcast.3.place, bf16[8,4,512,128]{3,2,1,0:T(8,128)(2,1)} %bitcast.32, ...), custom_call_target="tpu_custom_call" | custom-call | flops 2147483648 | bytes 16777216 | tf_op jit(solution)/shard_map/pallas_call | solution.py:367
  136.8 0.0 copy-done.2
  136.8 0.0 collective-permute-done.5.chip_ref
  136.8 13.6 %shard_map.75 = (bf16[8,4,512,128]{3,2,1,0:T(8,128)(2,1)}, f32[8,512,128]{2,1,0:T(8,128)}) custom-call(s32[32]{0:T(128)S(1)} %get-tuple-element.382, s32[8]{0:T(128)S(1)} %get-tuple-element.383, s32[32]{0:T(128)} %reshape.77.slashes, s32[8]{0:T(128)} %slash_count.3, s32[1]{0:T(128)} %bitcast.3.place, ...), custom_call_target="tpu_custom_call", output_to_operand_aliasing={{0}: (10, {}), {1}: (11, {})} | custom-call | flops 2147483648 | bytes 16777216 | tf_op jit(solution)/shard_map/pallas_call | solution.py:367
  150.4 11.6 %shard_map.78.rest_0_ = bf16[512,32,128]{2,1,0:T(8,128)(2,1)} custom-call(s32[32]{0:T(128)S(1)} %get-tuple-element.382, s32[8]{0:T(128)S(1)} %get-tuple-element.383, s32[2]{0:T(128)} %get-tuple-element.288.place, bf16[8,4,512,128]{3,2,1,0:T(8,128)(2,1)} %bitcast.34, bf16[8,4,512,128]{3,2,1,0:T(8,128)(2,1)} %get-tuple-element.265.part_ref, ...), custom_call_target="tpu_custom_call" | custom-call | flops 2147483648 | bytes 16777216 | tf_op jit(solution)/shard_map/pallas_call | solution.py:404
  162.0 0.0 collective-permute-done.10.tiles_ref
  162.0 11.5 %shard_map.79 = bf16[512,32,128]{2,1,0:T(8,128)(2,1)} custom-call(s32[32]{0:T(128)S(1)} %get-tuple-element.382, s32[8]{0:T(128)S(1)} %get-tuple-element.383, s32[2]{0:T(128)} %get-tuple-element.287.place, bf16[8,4,512,128]{3,2,1,0:T(8,128)(2,1)} %bitcast.35, bf16[8,4,512,128]{3,2,1,0:T(8,128)(2,1)} %get-tuple-element.265.part_ref, ...), custom_call_target="tpu_custom_call", output_to_operand_aliasing={{}: (7, {})} | custom-call | flops 2147483648 | bytes 16777216 | tf_op jit(solution)/shard_map/pallas_call | solution.py:404
  (3 shorter events, 0.0 us)
Async XLA Ops:
  0.0 2.4 %copy-start.5 = (bf16[512,8,128]{2,1,0:T(8,128)(2,1)S(1)}, bf16[512,8,128]{2,1,0:T(8,128)(2,1)}, u32[]{:S(2)}) copy-start(bf16[512,8,128]{2,1,0:T(8,128)(2,1)} %param.11) | copy-start | bytes 3145732
  0.9 2.5 %copy-start.7 = (s32[8]{0:T(128)S(1)}, s32[8]{0:T(128)}, u32[]{:S(2)}) copy-start(s32[8]{0:T(128)} %vert_count.7) | copy-start | bytes 100
  5.7 16.5 %all-to-all-start.2 = ((bf16[8,6,32,128]{3,2,1,0:T(8,128)(2,1)}), bf16[8,6,32,128]{3,2,1,0:T(8,128)(2,1)S(1)}, u32[]{:S(2)}, u32[]{:S(2)}) async-start(bf16[8,6,32,128]{3,2,1,0:T(8,128)(2,1)} %shard_map.73), calls=%async_computation.2 | async-start | bytes 786432 | tf_op jit(solution)/shard_map/all_to_all | solution.py:125
  22.1 0.7 copy-start.4
  25.7 18.8 %all-to-all-start.3 = ((bf16[8,6,32,128]{3,2,1,0:T(8,128)(2,1)}), bf16[8,6,32,128]{3,2,1,0:T(8,128)(2,1)S(1)}, u32[]{:S(2)}, u32[]{:S(2)}) async-start(bf16[8,6,32,128]{3,2,1,0:T(8,128)(2,1)} %shard_map.76), calls=%async_computation.3 | async-start | bytes 786432 | tf_op jit(solution)/shard_map/all_to_all | solution.py:128
  34.1 32.1 %collective-permute-start.6 = (bf16[4,4,256,128]{3,2,1,0:T(8,128)(2,1)}, bf16[4,4,256,128]{3,2,1,0:T(8,128)(2,1)}, u32[]{:S(2)}, u32[]{:S(2)}) collective-permute-start(bf16[4,4,256,128]{3,2,1,0:T(8,128)(2,1)} %bitcast.16), channel_id=1, source_target_pairs={{0,2},{2,4},{4,6},{6,8},{8,10},{10,12},{12,14},{14,0},{1,3},{3,5},... | collective-permute-start | bytes 3145736 | tf_op jit(solution)/shard_map/ppermute | solution.py:30
  35.6 50.2 %collective-permute-start.2 = (bf16[4,4,256,128]{3,2,1,0:T(8,128)(2,1)}, bf16[4,4,256,128]{3,2,1,0:T(8,128)(2,1)}, u32[]{:S(2)}, u32[]{:S(2)}) collective-permute-start(bf16[4,4,256,128]{3,2,1,0:T(8,128)(2,1)} %bitcast.15), channel_id=1, source_target_pairs={{14,30},{30,46},{46,62},{62,78},{78,94},{94,110},{110,126},{15,31}... | collective-permute-start | bytes 3145736 | tf_op jit(solution)/shard_map/ppermute | solution.py:30
  44.5 24.4 %copy-start.3 = (bf16[8,6,32,128]{3,2,1,0:T(8,128)(2,1)}, bf16[8,6,32,128]{3,2,1,0:T(8,128)(2,1)S(1)}, u32[]{:S(2)}) copy-start(bf16[8,6,32,128]{3,2,1,0:T(8,128)(2,1)S(1)} %all-to-all-done.3.same) | copy-start | bytes 1179652
  44.5 23.7 %collective-permute-start.9 = (bf16[8,6,32,128]{3,2,1,0:T(8,128)(2,1)S(1)}, bf16[8,6,32,128]{3,2,1,0:T(8,128)(2,1)S(1)}, u32[]{:S(2)}, u32[]{:S(2)}) collective-permute-start(bf16[8,6,32,128]{3,2,1,0:T(8,128)(2,1)S(1)} %all-to-all-done.3.same), channel_id=1, source_target_pairs={{0,1},{1,0},{2,3},{3,2},{4,5},{5,4},{6,7},{7,6},{8,9},{9,8},{10,11... | collective-permute-start | bytes 1179656 | tf_op jit(solution)/shard_map/ppermute | solution.py:117
  66.2 26.4 %collective-permute-start.7 = (bf16[4,4,256,128]{3,2,1,0:T(8,128)(2,1)}, bf16[4,4,256,128]{3,2,1,0:T(8,128)(2,1)}, u32[]{:S(2)}, u32[]{:S(2)}) collective-permute-start(bf16[4,4,256,128]{3,2,1,0:T(8,128)(2,1)} %collective-permute-done.6), channel_id=1, source_target_pairs={{0,16},{16,32},{32,48},{48,64},{64,80},{80,96},{96,112},{1,17},{17... | collective-permute-start | bytes 3145736 | tf_op jit(solution)/shard_map/ppermute | solution.py:30
  68.2 0.8 copy-start.6
  73.3 46.7 %all-to-all-start.4 = ((bf16[8,16,32,128]{3,2,1,0:T(8,128)(2,1)}), bf16[8,16,32,128]{3,2,1,0:T(8,128)(2,1)S(1)}, u32[]{:S(2)}, u32[]{:S(2)}) async-start(bf16[8,16,32,128]{3,2,1,0:T(8,128)(2,1)} %broadcast_in_dim.5), calls=%async_computation.4 | async-start | bytes 2097152 | tf_op jit(solution)/shard_map/all_to_all | solution.py:145
  83.5 24.6 %collective-permute-start.4 = (bf16[4,4,256,128]{3,2,1,0:T(8,128)(2,1)}, bf16[4,4,256,128]{3,2,1,0:T(8,128)(2,1)}, u32[]{:S(2)}, u32[]{:S(2)}) collective-permute-start(bf16[4,4,256,128]{3,2,1,0:T(8,128)(2,1)} %bitcast.15), channel_id=1, source_target_pairs={{0,2},{2,4},{4,6},{6,8},{8,10},{10,12},{12,14},{1,3},{3,5},{5,7},{... | collective-permute-start | bytes 3145736 | tf_op jit(solution)/shard_map/ppermute | solution.py:30
  85.8 26.5 %collective-permute-start.3 = (bf16[4,4,256,128]{3,2,1,0:T(8,128)(2,1)}, bf16[4,4,256,128]{3,2,1,0:T(8,128)(2,1)}, u32[]{:S(2)}, u32[]{:S(2)}) collective-permute-start(bf16[4,4,256,128]{3,2,1,0:T(8,128)(2,1)} %collective-permute-done.2), channel_id=1, source_target_pairs={{14,0},{15,1},{30,16},{31,17},{46,32},{47,33},{62,48},{63,49},{78,... | collective-permute-start | bytes 3145736 | tf_op jit(solution)/shard_map/ppermute | solution.py:34
  87.1 34.5 %collective-permute-start.1 = (bf16[8,4,256,128]{3,2,1,0:T(8,128)(2,1)S(1)}, bf16[8,4,256,128]{3,2,1,0:T(8,128)(2,1)}, u32[]{:S(2)}, u32[]{:S(2)}) collective-permute-start(bf16[8,4,256,128]{3,2,1,0:T(8,128)(2,1)S(1)} %bitcast.29), channel_id=1, source_target_pairs={{0,1},{2,3},{4,5},{6,7},{8,9},{10,11},{12,13},{14,15},{16,17},{18,... | collective-permute-start | bytes 6291464 | tf_op jit(solution)/shard_map/ppermute | solution.py:453
  94.9 25.1 %copy-start.8 = (s32[8,4]{0,1:T(4,128)S(1)}, s32[8,4]{0,1:T(4,128)}, u32[]{:S(2)}) copy-start(s32[8,4]{0,1:T(4,128)} %param.14) | copy-start | bytes 388
  94.9 26.6 %collective-permute-start.8 = (bf16[4,4,256,128]{3,2,1,0:T(8,128)(2,1)}, bf16[4,4,256,128]{3,2,1,0:T(8,128)(2,1)}, u32[]{:S(2)}, u32[]{:S(2)}) collective-permute-start(bf16[4,4,256,128]{3,2,1,0:T(8,128)(2,1)} %broadcast_select_fusion.far_ref), channel_id=1, source_target_pairs={{1,0},{3,2},{5,4},{7,6},{9,8},{11,10},{13,12},{15,14},{17,16},{19,... | collective-permute-start | bytes 3145736 | tf_op jit(solution)/shard_map/ppermute | solution.py:463
  114.6 22.2 %collective-permute-start.5 = (bf16[4,4,256,128]{3,2,1,0:T(8,128)(2,1)}, bf16[4,4,256,128]{3,2,1,0:T(8,128)(2,1)}, u32[]{:S(2)}, u32[]{:S(2)}) collective-permute-start(bf16[4,4,256,128]{3,2,1,0:T(8,128)(2,1)} %broadcast_select_fusion.1.far_ref), channel_id=1, source_target_pairs={{1,0},{3,2},{5,4},{7,6},{9,8},{11,10},{13,12},{15,14},{17,16},{19,... | collective-permute-start | bytes 3145736 | tf_op jit(solution)/shard_map/ppermute | solution.py:464
  120.0 16.8 %copy-start.2 = (bf16[8,16,32,128]{3,2,1,0:T(8,128)(2,1)}, bf16[8,16,32,128]{3,2,1,0:T(8,128)(2,1)S(1)}, u32[]{:S(2)}) copy-start(bf16[8,16,32,128]{3,2,1,0:T(8,128)(2,1)S(1)} %all-to-all-done.4.tiles_ref) | copy-start | bytes 3145732
  120.0 42.0 %collective-permute-start.10 = (bf16[8,16,32,128]{3,2,1,0:T(8,128)(2,1)S(1)}, bf16[8,16,32,128]{3,2,1,0:T(8,128)(2,1)}, u32[]{:S(2)}, u32[]{:S(2)}) collective-permute-start(bf16[8,16,32,128]{3,2,1,0:T(8,128)(2,1)S(1)} %all-to-all-done.4.tiles_ref), channel_id=1, source_target_pairs={{0,1},{1,0},{2,3},{3,2},{4,5},{5,4},{6,7},{7,6},{8,9},{9,8},{10,11... | collective-permute-start | bytes 3145736 | tf_op jit(solution)/shard_map/ppermute | solution.py:117
